TPU v7x, 128 devices: a whole 4x4x4 slice. The times are simulated.
128 devices in a mesh: pod: 1, data: 2 (over core), cp: 64 (over z, y, x).
Axes of the slice: x: 4, y: 4, z: 4, core: 2. Of those that a mesh axis runs over, the one named last changes fastest.
Arguments:
- c_latent: bfloat16 [2, 65536, 512], P(('pod', 'data'), 'cp')
- k_rope: bfloat16 [2, 65536, 64], P(('pod', 'data'), 'cp')
- queries: bfloat16 [2, 65536, 1, 192], P(('pod', 'data'), 'cp')
- w_uk: bfloat16 [512, 1, 128], replicated
- w_uv: bfloat16 [512, 1, 128], replicated
- d_out: bfloat16 [2, 65536, 1, 128], P(('pod', 'data'), 'cp')
Outputs:
- output 1: bfloat16 [2, 65536, 1, 128], P(('pod', 'data'), 'cp')
- output 2: float32 [2, 65536, 1, 192], P(('pod', 'data'), 'cp')
- output 3: float32 [2, 65536, 512], P(('pod', 'data'), 'cp')
- output 4: float32 [2, 65536, 64], P(('pod', 'data'), 'cp')
- output 5: float32 [512, 1, 128], P('pod')
- output 6: float32 [512, 1, 128], P('pod')
All inputs are finite; a program needn't handle non-finite values.
Results may differ from a plain program's by a relative error of at most 0.00698307.
Values are sent between devices in bfloat16 or wider.
A program may use at most 1 GiB of HBM per device.

v0:
```python
import jax
import jax.numpy as jnp
from jax import lax
from jax.sharding import PartitionSpec as P

NEG_BIG = -1.0e30


def block_scores(q_nope, q_rope, key_nope, key_rope, scale):
    nope_part = jnp.einsum('qhd,khd->hqk', q_nope, key_nope, preferred_element_type=jnp.float32)
    rope_part = jnp.einsum('qhe,ke->hqk', q_rope, key_rope, preferred_element_type=jnp.float32)
    return (nope_part + rope_part) * scale


def softmax_update(state, scores, values):
    row_max, row_sum, out_acc = state
    new_max = jnp.maximum(row_max, jnp.max(scores, axis=-1))
    weights = jnp.exp(scores - new_max[..., None])
    factor = jnp.exp(row_max - new_max)
    row_sum = row_sum * factor + jnp.sum(weights, axis=-1)
    out_acc = out_acc * factor[..., None] + jnp.einsum('hqk,khd->hqd', weights.astype(jnp.bfloat16), values, preferred_element_type=jnp.float32)
    return new_max, row_sum, out_acc


def block_grads(scores, log_sum, delta, q_nope, q_rope, grad_out, key_nope, key_rope, values, scale):
    weights = jnp.exp(scores - log_sum[..., None])
    d_weights = jnp.einsum('qhd,khd->hqk', grad_out, values, preferred_element_type=jnp.float32)
    d_scores = (weights * (d_weights - delta[..., None]) * scale).astype(jnp.bfloat16)
    weights_bf = weights.astype(jnp.bfloat16)
    dq_nope = jnp.einsum('hqk,khd->qhd', d_scores, key_nope, preferred_element_type=jnp.float32)
    dq_rope = jnp.einsum('hqk,ke->qhe', d_scores, key_rope, preferred_element_type=jnp.float32)
    dk_nope = jnp.einsum('hqk,qhd->khd', d_scores, q_nope, preferred_element_type=jnp.float32)
    dk_rope = jnp.einsum('hqk,qhe->ke', d_scores, q_rope, preferred_element_type=jnp.float32)
    d_values = jnp.einsum('hqk,qhd->khd', weights_bf, grad_out, preferred_element_type=jnp.float32)
    return dq_nope, dq_rope, dk_nope, dk_rope, d_values


def attention_core(queries, grad_out, nope_all, rope_all, values_all, my_index, ring):
    tok_dev, heads, qk_width = queries.shape
    n_nope = nope_all.shape[-1]
    n_val = values_all.shape[-1]
    half = tok_dev // 2
    scale = qk_width ** -0.5
    q_nope = queries[..., :n_nope]
    q_rope = queries[..., n_nope:]
    rows = jnp.arange(tok_dev)
    causal = rows[None, :] <= rows[:, None]

    def fetch(source):
        return (lax.dynamic_index_in_dim(nope_all, source, 0, keepdims=False), lax.dynamic_index_in_dim(rope_all, source, 0, keepdims=False), lax.dynamic_index_in_dim(values_all, source, 0, keepdims=False))

    own_nope, own_rope, own_values = fetch(my_index)
    start_state = (jnp.full((heads, tok_dev), NEG_BIG, jnp.float32), jnp.zeros((heads, tok_dev), jnp.float32), jnp.zeros((heads, tok_dev, n_val), jnp.float32))
    diag_scores = jnp.where(causal, block_scores(q_nope, q_rope, own_nope, own_rope, scale), NEG_BIG)
    state = softmax_update(start_state, diag_scores, own_values)

    def fwd_earlier(state, key_nope, key_rope, val_src):
        scores = block_scores(q_nope, q_rope, key_nope[:half], key_rope[:half], scale)
        return softmax_update(state, scores, val_src[:half])

    def fwd_later(state, key_nope, key_rope, val_src):
        scores = block_scores(q_nope[half:], q_rope[half:], key_nope, key_rope, scale)
        part_state = tuple(item[:, half:] for item in state)
        new_part = softmax_update(part_state, scores, val_src)
        return tuple(lax.dynamic_update_slice_in_dim(item, fresh, half, axis=1) for item, fresh in zip(state, new_part))

    def fwd_round(step, state):
        source = (my_index + step) % ring
        key_nope, key_rope, val_src = fetch(source)
        return lax.cond(source < my_index, fwd_earlier, fwd_later, state, key_nope, key_rope, val_src)

    row_max, row_sum, out_acc = lax.fori_loop(1, ring, fwd_round, state)
    out_f32 = out_acc / row_sum[..., None]
    log_sum = row_max + jnp.log(row_sum)
    delta = jnp.sum(jnp.swapaxes(grad_out.astype(jnp.float32), 0, 1) * out_f32, axis=-1)
    attn_out = jnp.swapaxes(out_f32, 0, 1).astype(jnp.bfloat16)

    diag_grads = block_grads(diag_scores, log_sum, delta, q_nope, q_rope, grad_out, own_nope, own_rope, own_values, scale)
    carry = (diag_grads[0], diag_grads[1], lax.dynamic_update_index_in_dim(jnp.zeros(nope_all.shape, jnp.float32), diag_grads[2], my_index, 0), lax.dynamic_update_index_in_dim(jnp.zeros(rope_all.shape, jnp.float32), diag_grads[3], my_index, 0), lax.dynamic_update_index_in_dim(jnp.zeros(values_all.shape, jnp.float32), diag_grads[4], my_index, 0))

    def bwd_earlier(carry, key_nope, key_rope, val_src, source):
        dq_nope, dq_rope, dk_nope_all, dk_rope_all, dv_all = carry
        scores = block_scores(q_nope, q_rope, key_nope[:half], key_rope[:half], scale)
        grads = block_grads(scores, log_sum, delta, q_nope, q_rope, grad_out, key_nope[:half], key_rope[:half], val_src[:half], scale)
        return (dq_nope + grads[0], dq_rope + grads[1], lax.dynamic_update_slice(dk_nope_all, grads[2][None], (source, 0, 0, 0)), lax.dynamic_update_slice(dk_rope_all, grads[3][None], (source, 0, 0)), lax.dynamic_update_slice(dv_all, grads[4][None], (source, 0, 0, 0)))

    def bwd_later(carry, key_nope, key_rope, val_src, source):
        dq_nope, dq_rope, dk_nope_all, dk_rope_all, dv_all = carry
        scores = block_scores(q_nope[half:], q_rope[half:], key_nope, key_rope, scale)
        grads = block_grads(scores, log_sum[:, half:], delta[:, half:], q_nope[half:], q_rope[half:], grad_out[half:], key_nope, key_rope, val_src, scale)
        return (lax.dynamic_update_slice_in_dim(dq_nope, dq_nope[half:] + grads[0], half, axis=0), lax.dynamic_update_slice_in_dim(dq_rope, dq_rope[half:] + grads[1], half, axis=0), lax.dynamic_update_index_in_dim(dk_nope_all, grads[2], source, 0), lax.dynamic_update_index_in_dim(dk_rope_all, grads[3], source, 0), lax.dynamic_update_index_in_dim(dv_all, grads[4], source, 0))

    def bwd_round(step, carry):
        source = (my_index + step) % ring
        key_nope, key_rope, val_src = fetch(source)
        return lax.cond(source < my_index, bwd_earlier, bwd_later, carry, key_nope, key_rope, val_src, source)

    dq_nope, dq_rope, dk_nope_all, dk_rope_all, dv_all = lax.fori_loop(1, ring, bwd_round, carry)
    grad_q = jnp.concatenate([dq_nope, dq_rope], axis=-1)
    return attn_out, grad_q, dk_nope_all, dk_rope_all, dv_all


def solution(mesh):
    ring = mesh.shape['cp']
    token_spec = P(('pod', 'data'), 'cp', None)
    head_spec = P(('pod', 'data'), 'cp', None, None)
    weight_spec = P(None, None, None)
    sum_spec = P('pod', None, None)

    def per_device(c_latent, k_rope, queries, w_uk, w_uv, d_out):
        my_index = lax.axis_index('cp')
        latent_seq = c_latent[0]
        key_nope = jnp.einsum('tl,lhd->thd', latent_seq, w_uk, preferred_element_type=jnp.float32).astype(jnp.bfloat16)
        values = jnp.einsum('tl,lhd->thd', latent_seq, w_uv, preferred_element_type=jnp.float32).astype(jnp.bfloat16)
        nope_all = lax.all_gather(key_nope, 'cp')
        rope_all = lax.all_gather(k_rope[0], 'cp')
        values_all = lax.all_gather(values, 'cp')
        attn_out, grad_q, dk_nope_all, dk_rope_all, dv_all = attention_core(queries[0], d_out[0], nope_all, rope_all, values_all, my_index, ring)
        dk_nope = lax.psum_scatter(dk_nope_all, 'cp', scatter_dimension=0, tiled=False)
        grad_rope = lax.psum_scatter(dk_rope_all, 'cp', scatter_dimension=0, tiled=False)
        d_values = lax.psum_scatter(dv_all, 'cp', scatter_dimension=0, tiled=False)
        grad_latent = jnp.einsum('thd,lhd->tl', dk_nope, w_uk, preferred_element_type=jnp.float32) + jnp.einsum('thd,lhd->tl', d_values, w_uv, preferred_element_type=jnp.float32)
        grad_w_uk = lax.psum(jnp.einsum('tl,thd->lhd', latent_seq, dk_nope, preferred_element_type=jnp.float32), ('data', 'cp'))
        grad_w_uv = lax.psum(jnp.einsum('tl,thd->lhd', latent_seq, d_values, preferred_element_type=jnp.float32), ('data', 'cp'))
        return attn_out[None], grad_q[None], grad_latent[None], grad_rope[None], grad_w_uk, grad_w_uv

    return jax.shard_map(per_device, mesh=mesh, in_specs=(token_spec, token_spec, head_spec, weight_spec, weight_spec, head_spec), out_specs=(head_spec, head_spec, token_spec, token_spec, sum_spec, sum_spec), check_vma=False)
```

profile of v0, /device:TPU:0, one launch (start us, length us, event | category | flops | bytes accessed | tf_op | source)
XLA Modules:
  0.0 2753.5 jit_solution(17430554683957095182)
XLA Ops:
  14.7 76.7 %all-gather.6.cloned.1.call-done = bf16[64,1024,64]{1,2,0:T(8,128)(2,1)} async-done(((bf16[1,1024,64]{1,2,0:T(8,128)(2,1)}), bf16[64,1024,64]{1,2,0:T(8,128)(2,1)}) %all-gather.6.cloned.1.call-update) | async-done | bytes 8388624 | tf_op jit(solution)/shard_map/all_gather | solution.py:116
  91.5 15.6 copy.45
  107.1 91.4 %all-gather.8.cloned.1.call-done = bf16[65536,128]{1,0:T(8,128)(2,1)} async-done(((bf16[1024,128]{1,0:T(8,128)(2,1)}), bf16[65536,128]{1,0:T(8,128)(2,1)}) %all-gather.8.cloned.1.call-update) | async-done | bytes 16777232 | tf_op jit(solution)/shard_map/all_gather | solution.py:115
  204.4 101.0 %all-gather.10.cloned.1.call-done = bf16[65536,128]{1,0:T(8,128)(2,1)} async-done(((bf16[1024,128]{1,0:T(8,128)(2,1)}), bf16[65536,128]{1,0:T(8,128)(2,1)}) %all-gather.10.cloned.1.call-update) | async-done | bytes 16777232 | tf_op jit(solution)/shard_map/all_gather | solution.py:117
  308.5 424.5 %while.42 = (s32[]{:T(128)}, f32[1,1024]{1,0:T(1,128)S(1)}, f32[1,1024]{1,0:T(1,128)S(1)}, f32[1,1024,128]{2,1,0:T(8,128)S(1)}, s32[]{:T(128)}, /*index=5*/bf16[...) while((s32[]{:T(128)}, f32[1,1024]{1,0:T(1,128)S(1)}, ...), condition=%wide.region_9.10_spmd, body=%wide.region_2.9_spmd.sunk | while | flops 339478560 | bytes 13697486 | solution.py:72
  743.2 11.2 broadcast.92.clone
  765.1 9.6 copy-done.1
  774.7 509.8 %while.43 = (s32[]{:T(128)}, f32[1024,1,128]{2,0,1:T(8,128)S(1)}, f32[1024,1,64]{0,2,1:T(8,128)S(1)}, f32[64,1024,1,128]{3,1,2,0:T(8,128)}, f32[64,1024,64]{1,2,...) while((s32[]{:T(128)}, f32[1024,1,128]{2,0,1:T(8,128)S(1)}, ...), condition=%wide.region_14.15_spmd, body=%wide.region_11.14_spmd.sunk | while | flops 876806144 | bytes 21242516 | solution.py:98
  776.7 6.1 conditional.5
  784.9 6.0 conditional.5
  792.9 6.1 conditional.5
  825.2 6.0 conditional.5
  841.4 6.1 conditional.5
  857.6 6.0 conditional.5
  865.7 6.1 conditional.5
  890.0 6.1 conditional.5
  898.1 6.1 conditional.5
  914.3 6.0 conditional.5
  922.4 6.1 conditional.5
  954.7 6.1 conditional.5
  962.8 6.1 conditional.5
  970.9 6.1 conditional.5
  979.0 6.0 conditional.5
  1003.2 6.0 conditional.5
  1011.3 6.1 conditional.5
  1035.6 6.1 conditional.5
  1043.7 6.0 conditional.5
  1059.9 6.1 conditional.5
  1084.1 6.1 conditional.5
  1100.3 6.1 conditional.5
  1116.5 6.0 conditional.5
  1124.6 6.1 conditional.5
  1132.7 6.1 conditional.5
  1148.9 6.1 conditional.5
  1157.0 6.1 conditional.5
  1181.3 6.1 conditional.5
  1189.4 6.1 conditional.5
  1221.7 6.1 conditional.5
  1229.8 6.1 conditional.5
  1237.9 6.1 conditional.5
  1246.0 6.0 conditional.5
  1262.2 6.1 conditional.5
  1270.3 6.1 conditional.5
  1278.4 6.1 conditional.5
  1285.1 472.0 %reduce-scatter.4.cloned.1.call-done = f32[1,1024,1,128]{3,1,2,0:T(8,128)} async-done(((f32[64,1024,1,128]{3,1,2,0:T(8,128)}), f32[1,1024,1,128]{3,1,2,0:T(8,128)}) %reduce-scatter.4.cloned.1.call-update) | async-done | bytes 524304 | tf_op jit(solution)/shard_map/reduce_scatter | solution.py:119
  1759.2 443.7 %reduce-scatter.6.cloned.1.call-done = f32[1,1024,1,128]{3,1,2,0:T(8,128)} async-done(((f32[64,1024,1,128]{3,1,2,0:T(8,128)}), f32[1,1024,1,128]{3,1,2,0:T(8,128)}) %reduce-scatter.6.cloned.1.call-update) | async-done | bytes 524304 | tf_op jit(solution)/shard_map/reduce_scatter | solution.py:121
  2210.2 144.2 %all-reduce.3.cloned.1.call-done = (f32[512,1,128]{0,2,1:T(8,128)}, f32[512,1,128]{0,2,1:T(8,128)}) async-done(((f32[512,1,128]{0,2,1:T(8,128)}, f32[512,1,128]{0,2,1:T(8,128)}), (f32[512,1,128]{0,2,1:T(8,128)}, f32[512,1,128]{0,2,1:T(8,128)})) %all-reduce.3.cloned.1.call-update) | async-done | bytes 524304 | tf_op jit(solution)/shard_map/psum | solution.py:123
  2357.9 388.8 %reduce-scatter.8.cloned.1.call-done = f32[1,1024,64]{1,2,0:T(8,128)} async-done(((f32[64,1024,64]{1,2,0:T(8,128)}), f32[1,1024,64]{1,2,0:T(8,128)}) %reduce-scatter.8.cloned.1.call-update) | async-done | bytes 262160 | tf_op jit(solution)/shard_map/reduce_scatter | solution.py:120
  (1543 shorter events, 1391.0 us)
Async XLA Ops:
  7.2 1.2 copy-start
  7.2 84.3 %all-gather.6.cloned.1.call-start = ((), (), s32[]{:S(2)}) async-start(), calls=%async_computation.3 | async-start | bytes 8519680 | tf_op jit(solution)/shard_map/all_gather | solution.py:116
  7.9 190.5 %all-gather.8.cloned.1.call-start = ((), (), s32[]{:S(2)}) async-start(), calls=%async_computation.7 | async-start | bytes 17039360 | tf_op jit(solution)/shard_map/all_gather | solution.py:115
  10.5 295.0 %all-gather.10.cloned.1.call-start = ((), (), s32[]{:S(2)}) async-start(), calls=%async_computation.8 | async-start | bytes 17039360 | tf_op jit(solution)/shard_map/all_gather | solution.py:117
  12.6 1744.5 %reduce-scatter.4.cloned.1.call-start = ((), (), s32[]{:S(2)}) async-start(), calls=%async_computation.4 | async-start | bytes 34078720 | tf_op jit(solution)/shard_map/reduce_scatter | solution.py:119
  14.7 183.7 %copy-start.8 = (bf16[1,1024,1,192]{1,3,2,0:T(8,128)(2,1)S(1)}, bf16[1,1024,1,192]{1,3,2,0:T(8,128)(2,1)}, u32[]{:S(2)}) copy-start(bf16[1,1024,1,192]{1,3,2,0:T(8,128)(2,1)} %param.16) | copy-start | bytes 1179652
  201.8 1.9 copy-start.2
  308.5 424.5 %copy-start.4 = (bf16[1,1024,1,128]{3,1,2,0:T(8,128)(2,1)S(1)}, bf16[1,1024,1,128]{3,1,2,0:T(8,128)(2,1)}, u32[]{:S(2)}) copy-start(bf16[1,1024,1,128]{3,1,2,0:T(8,128)(2,1)} %param.19) | copy-start | bytes 786436
  737.3 1.3 copy-start.6
  740.2 2.2 copy-start.7
  743.1 15.7 copy-start.5
  760.4 2.4 copy-start.3
  763.6 11.1 copy-start.1
  1284.5 918.4 %reduce-scatter.6.cloned.1.call-start = ((), (), s32[]{:S(2)}) async-start(), calls=%async_computation.5 | async-start | bytes 34078720 | tf_op jit(solution)/shard_map/reduce_scatter | solution.py:121
  1285.1 1069.3 %all-reduce.3.cloned.1.call-start = ((), (), s32[]{:S(2)}) async-start(), calls=%async_computation.9 | async-start | bytes 1048576 | tf_op jit(solution)/shard_map/psum | solution.py:123
  2205.0 541.7 %reduce-scatter.8.cloned.1.call-start = ((), (), s32[]{:S(2)}) async-start(), calls=%async_computation.6 | async-start | bytes 17039360 | tf_op jit(solution)/shard_map/reduce_scatter | solution.py:120
  2205.0 1.9 copy-start.11
  2205.7 2.7 copy-start.9
  2205.7 2.7 copy-start.10
Sparse Core Ops, SparseCore 0:
  10.9 80.5 all-gather.5
  94.9 103.4 all-gather.7
  201.9 103.4 all-gather.9
  1284.6 472.4 reduce-scatter.3
  1759.3 443.4 reduce-scatter.5
  2208.2 146.0 all-reduce.2
  2357.3 389.3 reduce-scatter.7
where the time goes:
time: 2770 us; the launch traced here: 2750 us
  waiting for transfers between devices  1720 us (62%)
  matrix products  502 us (18%)
  local copies, waits for them, and re-layouts  393 us (14%)
  other arithmetic  115 us (4%)
    reduce_scatter x1, waiting for transfers between devices, per_device(): lax.psum_scatter(dk_nope_all, 'cp', scatter_dimension=0, tiled=False)  472 us
    reduce_scatter x1, waiting for transfers between devices, per_device(): d_values = lax.psum_scatter(dv_all, 'cp', scatter_dimension=0, tiled=False)  444 us
    reduce_scatter x1, waiting for transfers between devices, per_device(): lax.psum_scatter(dk_rope_all, 'cp', scatter_dimension=0, tiled=False)  389 us
    psum x1, waiting for transfers between devices, per_device(): lax.psum(jnp.einsum('tl,thd->lhd', latent_seq, dk_nope, preferred_element...  144 us
    squeeze x126, local copies, waits for them, and re-layouts, fetch(): lax.dynamic_index_in_dim(values_all, source, 0, keepdims=False)  135 us
    squeeze x126, local copies, waits for them, and re-layouts, fetch(): lax.dynamic_index_in_dim(rope_all, source, 0, keepdims=False)  122 us
    all_gather x1, waiting for transfers between devices, per_device(): values_all = lax.all_gather(values, 'cp')  101 us
    all_gather x1, waiting for transfers between devices, per_device(): nope_all = lax.all_gather(key_nope, 'cp')  91.4 us
  transfers between devices with their start and end apart: 7, of which 7 were waited for; matrix products, arithmetic and copies ran while one was open for 1% of the time, Pallas kernels for 0%

commit v1 on v0

v1 whole, which is shorter than its diff:
```python
import functools

import jax
import jax.numpy as jnp
from jax import lax
from jax.experimental import pallas as pl
from jax.experimental.pallas import tpu as pltpu
from jax.sharding import PartitionSpec as P

BF = jnp.bfloat16
F32 = jnp.float32
NEG_BIG = -1.0e30
HALF = 512
NOPE = 128
ROPE = 64
QK = NOPE + ROPE
VAL = 128
AUG = 16
SCALE = QK ** -0.5
EXP2_SCALE = SCALE * 1.4426950408889634


def mm(a, b):
    return jnp.dot(a, b, preferred_element_type=F32)


def gray(r):
    return r ^ (r >> 1)


def core_kernel(qn_in, qr_in, kn_in, kr_in, vt_in, do_in,
                o_recv, dq_recv, dk_recv, dv_recv,
                q_s, qr_s, k_s, kr_s, vt_s, do_s, qt_s, kt_s, dot_s,
                ot_s, m_s, l_s, dq_s, dqr_s, dk_s, dv_s, st_s, st_r,
                sc0, sc1, dp0, dp1, pr0, pr1, ds0, ds1,
                q_send, q_recv_sem, k_send, k_recv_sem, do_send, do_recv_sem,
                st_send, st_recv_sem, o_send, o_recv_sem, dq_send, dq_recv_sem, dk_send, dk_recv_sem, own_sem):
    me = lax.axis_index('cp')
    x = me % 4
    y0 = (me // 4) % 2
    y1 = (me // 8) % 2
    z = me // 16
    row = me // 8
    col = me % 8

    def row_slot(rank):
        return 4 * (y0 ^ (rank // 4)) + (x + gray(rank % 4)) % 4

    def col_slot(rank):
        return 2 * ((z + gray(rank % 4)) % 4) + (y1 ^ (rank // 4))

    def row_dev(rank):
        return {'cp': 8 * row + row_slot(rank)}

    def col_dev(rank):
        return {'cp': 8 * col_slot(rank) + col}

    barrier = pltpu.get_barrier_semaphore()
    for r in range(1, 8):
        pl.semaphore_signal(barrier, inc=1, device_id=row_dev(r))
        pl.semaphore_signal(barrier, inc=1, device_id=col_dev(r))
    pl.semaphore_wait(barrier, 14)

    def q_copies(n, src_n, src_r, slot, dev):
        return [
            pltpu.make_async_remote_copy(src_n, q_s.at[slot, :, :, pl.ds(0, NOPE)], q_send.at[0, n], q_recv_sem.at[0, slot], device_id=dev),
            pltpu.make_async_remote_copy(src_r, qr_s.at[slot], q_send.at[1, n], q_recv_sem.at[1, slot], device_id=dev),
        ]

    def k_copies(n, src_n, src_r, src_v, slot, dev):
        return [
            pltpu.make_async_remote_copy(src_n, k_s.at[slot, :, :, pl.ds(0, NOPE)], k_send.at[0, n], k_recv_sem.at[0, slot], device_id=dev),
            pltpu.make_async_remote_copy(src_r, kr_s.at[slot], k_send.at[1, n], k_recv_sem.at[1, slot], device_id=dev),
            pltpu.make_async_remote_copy(src_v, vt_s.at[slot, :, pl.ds(0, VAL)], k_send.at[2, n], k_recv_sem.at[2, slot], device_id=dev),
        ]

    def do_copies(n, src, slot, dev):
        return [pltpu.make_async_remote_copy(src, do_s.at[slot, :, :, pl.ds(0, VAL)], do_send.at[n], do_recv_sem.at[slot], device_id=dev)]

    def own_q(n):
        return q_copies(n, qn_in, qr_in, col, row_dev(n + 1))

    def own_k(n):
        return k_copies(n, kn_in, kr_in, vt_in, row, col_dev(n + 1))

    def own_do(n):
        return do_copies(n, do_in, col, row_dev(n + 1))

    def pair_q(n):
        s = row_slot(4)
        return q_copies(4 + n, q_s.at[s, :, :, pl.ds(0, NOPE)], qr_s.at[s], s, row_dev(n + 1))

    def pair_k(n):
        s = col_slot(4)
        return k_copies(4 + n, k_s.at[s, :, :, pl.ds(0, NOPE)], kr_s.at[s], vt_s.at[s, :, pl.ds(0, VAL)], s, col_dev(n + 1))

    def pair_do(n):
        s = row_slot(4)
        return do_copies(4 + n, do_s.at[s, :, :, pl.ds(0, VAL)], s, row_dev(n + 1))

    def start(copies):
        for c in copies:
            c.start()

    for n in (3, 0, 1, 2):
        start(own_q(n))
        start(own_k(n))
    for n in (3, 0, 1, 2):
        start(own_do(n))

    ones = jnp.where(lax.broadcasted_iota(jnp.int32, (AUG, HALF), 0) < 3, 1.0, 0.0).astype(BF)

    def clear(s, _):
        for h in range(2):
            ot_s[s, h] = jnp.zeros((VAL, HALF), F32)
            dq_s[s, h] = jnp.zeros((HALF, QK), F32)
            dk_s[s, h] = jnp.zeros((QK, HALF), F32)
            dv_s[s, h] = jnp.zeros((VAL, HALF), F32)
            m_s[s, h] = jnp.full((1, HALF), NEG_BIG, F32)
            l_s[s, h] = jnp.zeros((1, HALF), F32)
            kt_s[s, h, QK:QK + AUG] = ones
            vt_s[s, h, VAL:VAL + AUG] = ones
        return 0

    def place_q(s, h):
        q_s[s, h, :, NOPE:QK] = qr_s[s, :, h * ROPE:(h + 1) * ROPE]
        qt_s[s, h] = q_s[s, h, :, 0:QK].T

    def place_k(s, h):
        k_s[s, h, :, NOPE:QK] = kr_s[s, :, h * ROPE:(h + 1) * ROPE]
        kt_s[s, h, 0:QK] = k_s[s, h].T

    def place_do(s):
        for h in range(2):
            dot_s[s, h] = do_s[s, h, :, 0:VAL].T

    q_s[col, :, :, 0:NOPE] = qn_in[...]
    qr_s[col] = qr_in[...]
    k_s[row, :, :, 0:NOPE] = kn_in[...]
    kr_s[row] = kr_in[...]
    vt_s[row, :, 0:VAL] = vt_in[...]
    do_s[col, :, :, 0:VAL] = do_in[...]
    for h in range(2):
        place_q(col, h)
        place_k(row, h)
    place_do(col)
    lax.fori_loop(0, 8, clear, 0)

    def wait_q(rank):
        for c in q_copies(0, qn_in, qr_in, row_slot(rank), row_dev(1)):
            c.wait_recv()

    def wait_k(rank):
        for c in k_copies(0, kn_in, kr_in, vt_in, col_slot(rank), col_dev(1)):
            c.wait_recv()

    def wait_do(rank):
        for c in do_copies(0, do_in, row_slot(rank), row_dev(1)):
            c.wait_recv()

    def low_pair(ks, qs):
        return jnp.where((ks < row) | ((ks == row) & (col <= qs)), 0, 1)

    def f_rank(t):
        late = t >= 40
        u = jnp.where(late, t - 40, t)
        mid = t >= 20
        v = jnp.where(mid, t - 20, t)
        a = jnp.where(late, 5 + u // 8, v // 4)
        b = jnp.where(late, u % 8, jnp.where(mid, 4, 0) + v % 4)
        return a, b

    def f_block(t, second):
        a, b = f_rank(t)
        ks, qs = col_slot(a), row_slot(b)
        if not second:
            return ks, qs, 0, 1
        h = low_pair(ks, qs)
        return ks, qs, h, h

    def f_scores(sc, blk):
        ks, qs, kh, qh = blk
        sc[...] = mm(k_s[ks, kh], qt_s[qs, qh])

    def f_soft(s, qs, qh):
        m0 = m_s[qs, qh]
        m1 = jnp.maximum(m0, jnp.max(s, axis=0, keepdims=True))
        p = jnp.exp2((s - m1) * EXP2_SCALE)
        alpha = jnp.exp2((m0 - m1) * EXP2_SCALE)
        l_s[qs, qh] = l_s[qs, qh] * alpha + jnp.sum(p, axis=0, keepdims=True)
        m_s[qs, qh] = m1
        return p.astype(BF), alpha

    def f_use(sc, blk, mask=False):
        ks, qs, kh, qh = blk
        s = sc[...]
        if mask:
            keys = lax.broadcasted_iota(jnp.int32, (HALF, HALF), 0)
            rows = lax.broadcasted_iota(jnp.int32, (HALF, HALF), 1)
            s = jnp.where(keys <= rows, s, NEG_BIG)
        p, alpha = f_soft(s, qs, qh)
        ot_s[qs, qh] = ot_s[qs, qh] * alpha + mm(vt_s[ks, kh, 0:VAL], p)

    for kh, qh in ((0, 0), (0, 1), (1, 1)):
        blk = (row, col, kh, qh)
        f_scores(sc0, blk)
        f_use(sc0, blk, mask=kh == qh)

    def stats_copy(slot, n):
        return pltpu.make_async_remote_copy(st_s.at[slot], st_r.at[slot, col], st_send.at[slot, n - 1], st_recv_sem.at[slot], device_id=row_dev(n))

    def send_stats(qs):
        for h in range(2):
            d = jnp.sum(ot_s[qs, h] * dot_s[qs, h].astype(F32), axis=0, keepdims=True)
            for j in range(4):
                c = slice(128 * j, 128 * j + 128)
                r = 4 * h + j
                st_s[qs, r:r + 1] = m_s[qs, h, :, c]
                st_s[qs, 8 + r:9 + r] = l_s[qs, h, :, c]
                st_s[qs, 16 + r:17 + r] = d[:, c]

    def start_stats(qs):
        for n in range(1, 8):
            stats_copy(qs, n).start()
        st_r[qs, col] = st_s[qs]

    def f_arrive(t):
        a, b = f_rank(t)
        first_q = (t < 4) | ((t >= 20) & (t < 24))
        first_k = ((t < 20) & (t % 4 == 0)) | ((t >= 40) & (t % 8 == 0))

        @pl.when(first_q & (b > 0) & (b != 4))
        def _():
            wait_q(b)

        @pl.when(first_q & (b > 0))
        def _():
            s = row_slot(b)
            for h in range(2):
                place_q(s, h)

        @pl.when(first_k & (a > 0) & (a != 4))
        def _():
            wait_k(a)

        @pl.when(first_k & (a > 0))
        def _():
            s = col_slot(a)
            for h in range(2):
                place_k(s, h)

        @pl.when(t == T_RELAY_Q)
        def _():
            wait_q(4)
            for n in range(3):
                start(pair_q(n))

        @pl.when(t == T_RELAY_K)
        def _():
            wait_k(4)
            for n in range(3):
                start(pair_k(n))

        @pl.when(t == T_RELAY_DO)
        def _():
            wait_do(4)
            for n in range(3):
                start(pair_do(n))
            place_do(row_slot(4))

        @pl.when((t >= 48) & (t < 56) & (b > 0))
        def _():
            @pl.when(b != 4)
            def _():
                wait_do(b)
                place_do(row_slot(b))

    f_arrive(1)
    f_scores(sc0, f_block(1, False))

    def f_step(t, _):
        nxt = jnp.minimum(t + 1, 63)

        @pl.when(t < 63)
        def _():
            f_arrive(nxt)

        b1, b2 = f_block(t, False), f_block(t, True)
        f_scores(sc1, b2)
        f_use(sc0, b1)
        f_scores(sc0, f_block(nxt, False))
        f_use(sc1, b2)

        @pl.when(t >= 57)
        def _():
            start_stats(row_slot(t - 57))

        @pl.when(t >= 56)
        def _():
            send_stats(row_slot(t - 56))
        return 0

    lax.fori_loop(1, 64, f_step, 0)
    start_stats(row_slot(7))

    def columns(v):
        flat = jnp.concatenate([v[j:j + 1] for j in range(4)], axis=1)
        hi = flat.astype(BF).astype(F32)
        mid = (flat - hi).astype(BF).astype(F32)
        lo = flat - hi - mid
        return jnp.concatenate([hi, mid, lo, jnp.zeros((AUG - 3, HALF), F32)], axis=0).T.astype(BF)

    def prepare(qs):
        pltpu.make_async_copy(st_r.at[qs, pl.ds(0, 7)], st_r.at[qs, pl.ds(0, 7)], st_recv_sem.at[qs]).wait()
        m = st_r[qs, :, 0:8]
        m_all = jnp.max(m, axis=0)
        w = jnp.exp2((m - m_all[None]) * EXP2_SCALE)
        l_all = jnp.sum(w * st_r[qs, :, 8:16], axis=0)
        inv = 1.0 / l_all
        delta = jnp.sum(w * st_r[qs, :, 16:24], axis=0) * inv
        lse = m_all + jnp.log2(l_all) * (1.0 / EXP2_SCALE)
        mine = jnp.exp2((st_s[qs, 0:8] - m_all) * EXP2_SCALE) * inv
        for h in range(2):
            q_s[qs, h, :, QK:QK + AUG] = columns(-lse[4 * h:4 * h + 4])
            do_s[qs, h, :, VAL:VAL + AUG] = columns(-delta[4 * h:4 * h + 4])
            for j in range(4):
                r = 4 * h + j
                c = slice(128 * j, 128 * j + 128)
                ot_s[qs, h, :, c] = ot_s[qs, h, :, c] * mine[r:r + 1]

    def o_copy(rank):
        s = row_slot(rank)
        return pltpu.make_async_remote_copy(ot_s.at[s], o_recv.at[col], o_send.at[rank], o_recv_sem.at[col], device_id=row_dev(rank))

    def b_rank(t):
        own = t >= 56
        return jnp.where(own, 0, 1 + t // 8), jnp.where(own, t - 55, t % 8)

    def b_block(t, second):
        a, b = b_rank(t)
        ks, qs = col_slot(a), row_slot(b)
        if not second:
            return ks, qs, 0, 1
        h = low_pair(ks, qs)
        return ks, qs, h, h

    def b_scores(sc, dp, blk):
        ks, qs, kh, qh = blk
        sc[...] = mm(q_s[qs, qh], kt_s[ks, kh])
        dp[...] = mm(do_s[qs, qh], vt_s[ks, kh])

    def b_elem(sc, dp, pr, ds, blk, mask=False):
        ks, qs, kh, qh = blk
        p = jnp.exp2(sc[...] * EXP2_SCALE)
        if mask:
            rows = lax.broadcasted_iota(jnp.int32, (HALF, HALF), 0)
            keys = lax.broadcasted_iota(jnp.int32, (HALF, HALF), 1)
            p = jnp.where(keys <= rows, p, 0.0)
        pr[...] = p.astype(BF)
        ds[...] = (p * dp[...]).astype(BF)

    def b_grads(pr, ds, blk):
        ks, qs, kh, qh = blk
        p = pr[...]
        g = ds[...]
        dv_s[ks, kh] += mm(dot_s[qs, qh], p)
        dk_s[ks, kh] += mm(qt_s[qs, qh], g)
        dq_s[qs, qh] += mm(g, k_s[ks, kh])

    def dkv_copies(rank):
        s = col_slot(rank)
        dev = col_dev(rank)
        return [
            pltpu.make_async_remote_copy(dk_s.at[s], dk_recv.at[row], dk_send.at[0, rank], dk_recv_sem.at[0, row], device_id=dev),
            pltpu.make_async_remote_copy(dv_s.at[s], dv_recv.at[row], dk_send.at[1, rank], dk_recv_sem.at[1, row], device_id=dev),
        ]

    def dq_copies(rank):
        s = row_slot(rank)
        dev = row_dev(rank)
        return [
            pltpu.make_async_remote_copy(dq_s.at[s, :, :, pl.ds(0, NOPE)], dq_recv.at[col, pl.ds(0, 2)], dq_send.at[0, rank], dq_recv_sem.at[0, col], device_id=dev),
            pltpu.make_async_remote_copy(dqr_s.at[s], dq_recv.at[col, 2], dq_send.at[1, rank], dq_recv_sem.at[1, col], device_id=dev),
        ]

    def pack_dq(qs):
        dqr_s[qs, :, 0:ROPE] = dq_s[qs, 0, :, NOPE:QK]
        dqr_s[qs, :, ROPE:2 * ROPE] = dq_s[qs, 1, :, NOPE:QK]

    pr1[...] = jnp.zeros((HALF, HALF), BF)
    ds1[...] = jnp.zeros((HALF, HALF), BF)
    prepare(row_slot(0))
    b_scores(sc0, dp0, b_block(0, False))

    def b_step(t, _):
        @pl.when(t < 7)
        def _():
            prepare(row_slot(t + 1))

        b1, b2 = b_block(t, False), b_block(t, True)
        prev = b_block(jnp.maximum(t - 1, 0), True)
        nxt = b_block(jnp.minimum(t + 1, 62), False)
        b_scores(sc1, dp1, b2)
        b_elem(sc0, dp0, pr0, ds0, b1)
        b_grads(pr1, ds1, prev)
        b_scores(sc0, dp0, nxt)
        b_elem(sc1, dp1, pr1, ds1, b2)
        b_grads(pr0, ds0, b1)

        @pl.when((t >= 1) & (t < 8))
        def _():
            o_copy(t).start()

        @pl.when((t % 8 == 0) & (t > 0))
        def _():
            start(dkv_copies(t // 8))

        @pl.when(t >= 58)
        def _():
            start(dq_copies(t - 57))

        @pl.when(t >= 57)
        def _():
            pack_dq(row_slot(t - 56))
        return 0

    lax.fori_loop(0, 63, b_step, 0)
    b_grads(pr1, ds1, b_block(62, True))
    pack_dq(row_slot(7))
    for kh, qh in ((0, 0), (0, 1), (1, 1)):
        blk = (row, col, kh, qh)
        b_scores(sc0, dp0, blk)
        b_elem(sc0, dp0, pr0, ds0, blk, mask=kh == qh)
        b_grads(pr0, ds0, blk)
        if kh == 0 and qh == 0:
            start(dq_copies(6))
            start(dq_copies(7))
    pack_dq(col)

    own = [
        pltpu.make_async_copy(ot_s.at[col], o_recv.at[col], own_sem.at[0]),
        pltpu.make_async_copy(dq_s.at[col, :, :, pl.ds(0, NOPE)], dq_recv.at[col, pl.ds(0, 2)], own_sem.at[1]),
        pltpu.make_async_copy(dqr_s.at[col], dq_recv.at[col, 2], own_sem.at[2]),
        pltpu.make_async_copy(dk_s.at[row], dk_recv.at[row], own_sem.at[3]),
        pltpu.make_async_copy(dv_s.at[row], dv_recv.at[row], own_sem.at[4]),
    ]
    start(own)

    for n in range(4):
        for c in own_q(n) + own_k(n) + own_do(n):
            c.wait_send()
    for n in range(3):
        for c in pair_q(n) + pair_k(n) + pair_do(n):
            c.wait_send()
    for r in range(1, 8):
        for s in range(8):
            stats_copy(s, r).wait_send()
        o_copy(r).wait_send()
        for c in dkv_copies(r) + dq_copies(r):
            c.wait_send()
        s = row_slot(r)
        pltpu.make_async_remote_copy(ot_s.at[0], o_recv.at[s], o_send.at[r], o_recv_sem.at[s], device_id=row_dev(r)).wait_recv()
        pltpu.make_async_remote_copy(dq_s.at[0, :, :, pl.ds(0, NOPE)], dq_recv.at[s, pl.ds(0, 2)], dq_send.at[0, r], dq_recv_sem.at[0, s], device_id=row_dev(r)).wait_recv()
        pltpu.make_async_remote_copy(dqr_s.at[0], dq_recv.at[s, 2], dq_send.at[1, r], dq_recv_sem.at[1, s], device_id=row_dev(r)).wait_recv()
        s = col_slot(r)
        pltpu.make_async_remote_copy(dk_s.at[0], dk_recv.at[s], dk_send.at[0, r], dk_recv_sem.at[0, s], device_id=col_dev(r)).wait_recv()
        pltpu.make_async_remote_copy(dv_s.at[0], dv_recv.at[s], dk_send.at[1, r], dk_recv_sem.at[1, s], device_id=col_dev(r)).wait_recv()
    for c in own:
        c.wait()


T_RELAY_Q = 4
T_RELAY_K = 8
T_RELAY_DO = 40


def core_call(qn, qr, kn, kr, vt, do):
    vmem = pltpu.VMEM
    dma = pltpu.SemaphoreType.DMA
    n = 8
    scratch = [
        vmem((n, 2, HALF, QK + AUG), BF), vmem((n, HALF, 128), BF), vmem((n, 2, HALF, QK), BF), vmem((n, HALF, 128), BF),
        vmem((n, 2, VAL + AUG, HALF), BF), vmem((n, 2, HALF, VAL + AUG), BF),
        vmem((n, 2, QK, HALF), BF), vmem((n, 2, QK + AUG, HALF), BF), vmem((n, 2, VAL, HALF), BF),
        vmem((n, 2, VAL, HALF), F32), vmem((n, 2, 1, HALF), F32), vmem((n, 2, 1, HALF), F32),
        vmem((n, 2, HALF, QK), F32), vmem((n, HALF, 128), F32), vmem((n, 2, QK, HALF), F32), vmem((n, 2, VAL, HALF), F32),
        vmem((n, 24, 128), F32), vmem((n, n, 24, 128), F32),
        vmem((HALF, HALF), F32), vmem((HALF, HALF), F32), vmem((HALF, HALF), F32), vmem((HALF, HALF), F32),
        vmem((HALF, HALF), BF), vmem((HALF, HALF), BF), vmem((HALF, HALF), BF), vmem((HALF, HALF), BF),
                dma((2, 7)), dma((2, n)), dma((3, 7)), dma((3, n)), dma((7,)), dma((n,)),
        dma((n, 7)), dma((n,)), dma((n,)), dma((n,)), dma((2, n)), dma((2, n)), dma((2, n)), dma((2, n)), dma((5,)),
    ]
    return pl.pallas_call(
        core_kernel,
        out_shape=(
            jax.ShapeDtypeStruct((n, 2, VAL, HALF), F32),
            jax.ShapeDtypeStruct((n, 3, HALF, 128), F32),
            jax.ShapeDtypeStruct((n, 2, QK, HALF), F32),
            jax.ShapeDtypeStruct((n, 2, VAL, HALF), F32),
        ),
        in_specs=[pl.BlockSpec(memory_space=pltpu.VMEM)] * 6,
        out_specs=[pl.BlockSpec(memory_space=pl.ANY)] * 4,
        scratch_shapes=scratch,
        compiler_params=pltpu.CompilerParams(collective_id=0, has_side_effects=True, vmem_limit_bytes=67043328),
        name='core',
    )(qn, qr, kn, kr, vt, do)


def solution(mesh):
    token_spec = P(('pod', 'data'), 'cp', None)
    head_spec = P(('pod', 'data'), 'cp', None, None)
    weight_spec = P(None, None, None)
    sum_spec = P('pod', None, None)

    def per_device(c_latent, k_rope, queries, w_uk, w_uv, d_out):
        latent = c_latent[0]
        q = queries[0, :, 0, :]
        wk, wv = w_uk[:, 0, :], w_uv[:, 0, :]
        kn = mm(latent, wk).astype(BF).reshape(2, HALF, NOPE)
        vt = jnp.einsum('ld,htl->hdt', wv, latent.reshape(2, HALF, -1), preferred_element_type=F32).astype(BF)
        kr = jnp.concatenate([k_rope[0, :HALF], k_rope[0, HALF:]], axis=1)
        qn = q[:, :NOPE].reshape(2, HALF, NOPE)
        qr = jnp.concatenate([q[:HALF, NOPE:], q[HALF:, NOPE:]], axis=1)
        do = d_out[0, :, 0, :].reshape(2, HALF, VAL)
        o_parts, dq_parts, dk_parts, dv_parts = core_call(qn, qr, kn, kr, vt, do)
        attn_out = jnp.sum(o_parts, axis=0).transpose(0, 2, 1).astype(BF).reshape(1, 2 * HALF, 1, VAL)
        dq = jnp.sum(dq_parts, axis=0) * SCALE
        dq_rope = jnp.concatenate([dq[2, :, :ROPE], dq[2, :, ROPE:]], axis=0)
        grad_q = jnp.concatenate([dq[:2].reshape(2 * HALF, NOPE), dq_rope], axis=-1).reshape(1, 2 * HALF, 1, QK)
        dk = jnp.sum(dk_parts, axis=0) * SCALE
        dv = jnp.sum(dv_parts, axis=0)
        grad_rope = dk[:, NOPE:].transpose(0, 2, 1).reshape(1, 2 * HALF, ROPE)
        dkn = dk[:, :NOPE]
        grad_latent = (jnp.einsum('hdt,ld->htl', dkn, wk, preferred_element_type=F32) + jnp.einsum('hdt,ld->htl', dv, wv, preferred_element_type=F32)).reshape(1, 2 * HALF, -1)
        lat = latent.reshape(2, HALF, -1)
        grad_w_uk = lax.psum(jnp.einsum('htl,hdt->ld', lat, dkn, preferred_element_type=F32), ('data', 'cp'))
        grad_w_uv = lax.psum(jnp.einsum('htl,hdt->ld', lat, dv, preferred_element_type=F32), ('data', 'cp'))
        return attn_out, grad_q, grad_latent, grad_rope, grad_w_uk[:, None], grad_w_uv[:, None]

    return jax.shard_map(per_device, mesh=mesh, in_specs=(token_spec, token_spec, head_spec, weight_spec, weight_spec, head_spec), out_specs=(head_spec, head_spec, token_spec, token_spec, sum_spec, sum_spec), check_vma=False)
```

time: 2770 us -> 526 us (0.19)
  the two profiles are of different devices: /device:TPU:0 before, /device:TPU:1 now
where the time goes in v1:
time: 526 us
  Pallas kernels  346 us (66%)
  waiting for transfers between devices  129 us (25%)
  other arithmetic  16.2 us (3%)
  between operations  14.2 us (3%)
  local copies, waits for them, and re-layouts  14 us (3%)
  matrix products  6.58 us (1%)
    pallas_call x1, Pallas kernels, core_call(): pl.pallas_call(core_kernel, out_shape=(jax.ShapeDtypeStruct((n, 2, VAL, H...  346 us
    psum x1, waiting for transfers between devices, per_device(): lax.psum(jnp.einsum('htl,hdt->ld', lat, dkn, preferred_element_type=F32),...  129 us
  transfers between devices with their start and end apart: 1, of which 1 were waited for; matrix products, arithmetic and copies ran while one was open for 3% of the time, Pallas kernels for 0%

profile of v1, /device:TPU:1, one launch (start us, length us, event | category | flops | bytes accessed | tf_op | source)
XLA Modules:
  0.0 526.0 jit_solution(12579489211968798497)
XLA Ops:
  7.2 0.0 copy-start.6
  7.2 0.0 copy-start
  7.2 0.0 copy-start.4
  7.2 0.0 all-reduce.3.cloned.1.call-start
  7.2 1.3 copy.42
  8.5 0.7 slice.40
  9.3 0.9 fusion.10
  10.2 0.1 copy.57
  10.3 0.1 copy.58
  10.4 0.0 copy-done.6
  10.4 0.0 copy-done
  10.4 1.1 convolution_convert_fusion.1
  11.6 0.0 copy-done.4
  11.6 1.2 fusion.vt_in
  12.8 0.8 pad_maximum_fusion
  13.6 345.8 %core.1 = (f32[8,2,128,512]{3,2,1,0:T(8,128)}, f32[8,3,512,128]{3,2,1,0:T(8,128)}, f32[8,2,192,512]{3,2,1,0:T(8,128)}, f32[8,2,128,512]{3,2,1,0:T(8,128)}) custom-call(bf16[2,512,128]{2,1,0:T(8,128)(2,1)} %bitcast.64, bf16[512,128]{1,0:T(8,128)(2,1)} %get-tuple-element.46.qr_in, bf16[2,512,128]{2,1,0:T(8,128)(2,1)} %bitcast.66, ...), custom_call_target="tpu_custom_call" | custom-call | tf_op jit(solution)/shard_map/core/pallas_call | solution.py:493
  359.4 0.0 copy-start.1
  359.4 2.8 reduce_sum.39
  362.2 0.0 copy-done.1
  362.2 1.0 convolution_bitcast_fusion
  363.2 3.6 reduce_sum.38
  366.8 0.3 copy.47
  367.2 0.1 broadcast_multiply_fusion
  367.3 0.0 copy-start.2
  367.3 1.0 convolution_bitcast_fusion.1
  368.3 0.0 all-reduce.3.cloned.1.call-update
  368.3 3.2 reduce_sum.37
  371.5 0.0 copy-start.7
  371.5 0.1 broadcast_multiply_fusion.1
  371.6 0.0 copy-start.3
  371.6 0.9 copy-done.3
  372.5 0.9 slice_bitcast_fusion.1
  373.4 0.0 copy-done.2
  373.4 0.0 copy-done.7
  373.4 0.4 fusion.3
  373.8 0.0 slice-start
  373.8 0.0 slice-start.1
  373.8 3.5 reduce_sum.36
  377.3 1.8 copy.46
  379.1 0.0 slice-done
  379.1 0.9 copy.51
  380.0 0.0 slice-done.1
  380.0 2.1 maximum_bitcast_fusion
  382.1 2.4 copy.50
  384.6 1.8 convolution_add_fusion
  386.3 129.3 %all-reduce.3.cloned.1.call-done = (f32[512,1,128]{0,2,1:T(8,128)}, f32[512,1,128]{0,2,1:T(8,128)}) async-done(((f32[512,1,128]{0,2,1:T(8,128)}, f32[512,1,128]{0,2,1:T(8,128)}), (f32[512,1,128]{0,2,1:T(8,128)}, f32[512,1,128]{0,2,1:T(8,128)})) %all-reduce.3.cloned.1.call-update) | async-done | bytes 524304 | tf_op jit(solution)/shard_map/psum | solution.py:536
  515.6 1.8 copy.52
  517.4 1.8 copy.53
  (3 shorter events, 0.0 us)
Async XLA Ops:
  7.2 3.3 copy-start.6
  7.2 3.3 copy-start
  7.2 4.4 copy-start.4
  7.2 508.4 %all-reduce.3.cloned.1.call-start = ((), (), s32[]{:S(2)}) async-start(), calls=%async_computation | async-start | bytes 1048576 | tf_op jit(solution)/shard_map/psum | solution.py:536
  359.4 2.8 copy-start.1
  367.3 6.1 %copy-start.2 = (f32[2,192,512]{1,2,0:T(8,128)}, f32[2,192,512]{1,2,0:T(8,128)S(1)}, u32[]{:S(2)}) copy-start(f32[2,192,512]{1,2,0:T(8,128)S(1)} %broadcast_multiply_fusion) | copy-start | bytes 2359300
  371.5 1.8 copy-start.7
  371.6 0.9 copy-start.3
  373.8 5.3 %slice-start = ((f32[2,192,512]{1,2,0:T(8,128)}), f32[2,64,512]{1,2,0:T(8,128)S(1)}, s32[]{:S(2)}) async-start(f32[2,192,512]{1,2,0:T(8,128)} %copy-done.2), calls=%async_computation.1 | async-start | bytes 1048576 | tf_op jit(solution)/shard_map/slice | solution.py:532
  373.8 6.2 %slice-start.1 = ((f32[3,512,128]{2,1,0:T(8,128)}), f32[2,512,128]{2,1,0:T(8,128)S(1)}, s32[]{:S(2)}) async-start(f32[3,512,128]{2,1,0:T(8,128)} %copy-done.3), calls=%async_computation.2 | async-start | bytes 1048576 | tf_op jit(solution)/shard_map/slice | solution.py:529
  380.0 4.5 copy-start.5
Sparse Core Ops, SparseCore 0:
  368.5 147.0 all-reduce.2

commit v2 on v1

v2 whole, which is shorter than its diff:
```python
import jax
import jax.numpy as jnp
from jax import lax
from jax.experimental import pallas as pl
from jax.experimental.pallas import tpu as pltpu
from jax.sharding import PartitionSpec as P

BF = jnp.bfloat16
F32 = jnp.float32
NEG_BIG = -1.0e30
HALF = 512
LATENT = 512
NOPE = 128
ROPE = 64
QK = NOPE + ROPE
VAL = 128
AUG = 16
SCALE = QK ** -0.5
EXP2_SCALE = SCALE * 1.4426950408889634
T_OWN_DO = 12
T_RELAY_Q = 9
T_RELAY_K = 9
T_RELAY_DO = 34
T_LAST = 56
T_PAIR_O = 38
T_PAIR_KV = 53


def mm(a, b):
    return jnp.dot(a, b, preferred_element_type=F32)


def mm_t(a, b):
    return lax.dot_general(a, b, (((1,), (1,)), ((), ())), preferred_element_type=F32)


def gray(r):
    return r ^ (r >> 1)


def order(n, ranks):
    out = ranks[-1]
    for i in range(len(ranks) - 2, -1, -1):
        out = jnp.where(n <= i, ranks[i], out)
    return out


def among(t, steps):
    out = t == steps[0]
    for v in steps[1:]:
        out = out | (t == v)
    return out


def at(t, steps, ranks):
    out = ranks[-1]
    for v, r in list(zip(steps, ranks))[-2::-1]:
        out = jnp.where(t <= v, r, out)
    return out


def core_kernel(c_in, kpe_in, q_in, wk_in, wv_in, do_in,
                out_o, out_q, out_c, out_r, out_uk, out_uv, xo, xq, xqv, zkv, zkvv, po, pq, pkv,
                q_s, qr_s, k_s, kr_s, vt_s, do_s, qt_s, kt_s, dot_s,
                ot_s, m_s, l_s, dq_s, dqr_s, dk_s, dv_s, st_s, st_r, stg, w_s, ws_r, wl_r, rope_s, q_out_s, wr_s, wr_r, wc_s, wc_r,
                sc0, sc1, dp0, dp1, pr0, pr1, ds0, ds1,
                q_send, q_recv, k_send, k_recv, do_send, do_recv, st_send, st_recv,
                xo_send, xo_recv, xq_send, xq_recv, xqv_send, xqv_recv, zkv_send, zkv_recv, zkvv_send, zkvv_recv, p_send, p_recv, loc, outs, w_send, w_recv):
    me = lax.axis_index('cp')
    core = lax.axis_index('data')
    x = me % 4
    y0 = (me // 4) % 2
    y1 = (me // 8) % 2
    z = me // 16
    row = me // 8
    col = me % 8

    def row_slot(rank):
        return 4 * (y0 ^ (rank // 4)) + (x + gray(rank % 4)) % 4

    def col_slot(rank):
        return 2 * ((z + gray(rank % 4)) % 4) + (y1 ^ (rank // 4))

    def row_dev(rank):
        return {'cp': 8 * row + row_slot(rank)}

    def col_dev(rank):
        return {'cp': 8 * col_slot(rank) + col}

    barrier = pltpu.get_barrier_semaphore()
    for r in range(1, 8):
        pl.semaphore_signal(barrier, inc=1, device_id=row_dev(r))
        pl.semaphore_signal(barrier, inc=1, device_id=col_dev(r))
    pl.semaphore_signal(barrier, inc=1, device_id={'data': 1 - core})

    wvt = wv_in[...].T
    for h in range(2):
        c = slice(h * HALF, (h + 1) * HALF)
        qt_s[col, h] = q_in[:, c]
        q = q_in[:, c].T
        q_s[col, h, :, 0:QK] = q
        qr_s[col, :, h * ROPE:(h + 1) * ROPE] = q[:, NOPE:QK]
        do_s[col, h, :, 0:VAL] = do_in[h]
    for h in range(2):
        k_s[row, h, :, 0:NOPE] = mm(c_in[h], wk_in[...]).astype(BF)
        rope = kpe_in[:, h * HALF:(h + 1) * HALF].T
        k_s[row, h, :, NOPE:QK + ROPE] = jnp.concatenate([rope, rope], axis=1)
        kr_s[row, :, h * ROPE:(h + 1) * ROPE] = rope
        vt_s[row, h, 0:VAL] = mm_t(wvt, c_in[h]).astype(BF)

    pl.semaphore_wait(barrier, 15)

    def q_copies(n, slot, dev):
        return [
            pltpu.make_async_remote_copy(q_s.at[slot, :, :, pl.ds(0, NOPE)], q_s.at[slot, :, :, pl.ds(0, NOPE)], q_send.at[0, n], q_recv.at[0, slot], device_id=dev),
            pltpu.make_async_remote_copy(qr_s.at[slot], qr_s.at[slot], q_send.at[1, n], q_recv.at[1, slot], device_id=dev),
        ]

    def k_copies(n, slot, dev):
        return [
            pltpu.make_async_remote_copy(k_s.at[slot, :, :, pl.ds(0, NOPE)], k_s.at[slot, :, :, pl.ds(0, NOPE)], k_send.at[0, n], k_recv.at[0, slot], device_id=dev),
            pltpu.make_async_remote_copy(kr_s.at[slot], kr_s.at[slot], k_send.at[1, n], k_recv.at[1, slot], device_id=dev),
            pltpu.make_async_remote_copy(vt_s.at[slot, :, pl.ds(0, VAL)], vt_s.at[slot, :, pl.ds(0, VAL)], k_send.at[2, n], k_recv.at[2, slot], device_id=dev),
        ]

    def do_copies(n, slot, dev):
        return [pltpu.make_async_remote_copy(do_s.at[slot, :, :, pl.ds(0, VAL)], do_s.at[slot, :, :, pl.ds(0, VAL)], do_send.at[n], do_recv.at[slot], device_id=dev)]

    def start(copies):
        for c in copies:
            c.start()

    for n in (3, 0, 1, 2):
        start(q_copies(n, col, row_dev(n + 1)))
        start(k_copies(n, row, col_dev(n + 1)))

    ones_row = jnp.where(lax.broadcasted_iota(jnp.int32, (AUG, HALF), 0) < 3, 1.0, 0.0).astype(BF)

    def clear(s, _):
        for h in range(2):
            ot_s[s, h] = jnp.zeros((VAL, HALF), F32)
            dq_s[s, h] = jnp.zeros((HALF, NOPE), F32)
            dk_s[s, h] = jnp.zeros((QK, HALF), F32)
            dv_s[s, h] = jnp.zeros((VAL, HALF), F32)
            m_s[s, h] = jnp.full((1, HALF), NEG_BIG, F32)
            l_s[s, h] = jnp.zeros((1, HALF), F32)
            kt_s[s, h, QK:QK + AUG] = ones_row
            vt_s[s, h, VAL:VAL + AUG] = ones_row
        dqr_s[s] = jnp.zeros((HALF, 128), F32)
        return 0

    def place_q(s):
        for h in range(2):
            q_s[s, h, :, NOPE:QK] = qr_s[s, :, h * ROPE:(h + 1) * ROPE]
            qt_s[s, h] = q_s[s, h, :, 0:QK].T

    def place_k(s):
        for h in range(2):
            rope = kr_s[s, :, h * ROPE:(h + 1) * ROPE]
            k_s[s, h, :, NOPE:QK + ROPE] = jnp.concatenate([rope, rope], axis=1)
            kt_s[s, h, 0:QK] = k_s[s, h, :, 0:QK].T

    def place_do(s):
        for h in range(2):
            dot_s[s, h] = do_s[s, h, :, 0:VAL].T

    for h in range(2):
        kt_s[row, h, 0:QK] = k_s[row, h, :, 0:QK].T
    place_do(col)
    lax.fori_loop(0, 8, clear, 0)

    def wait_q(rank):
        for c in q_copies(0, row_slot(rank), row_dev(1)):
            c.wait_recv()

    def wait_k(rank):
        for c in k_copies(0, col_slot(rank), col_dev(1)):
            c.wait_recv()

    def wait_do(rank):
        for c in do_copies(0, row_slot(rank), row_dev(1)):
            c.wait_recv()

    def two_blocks(ks, qs, second):
        if not second:
            return ks, qs, 0, 1
        h = jnp.where((ks < row) | ((ks == row) & (col <= qs)), 0, 1)
        return ks, qs, h, h

    f_rects = ((1, 0, 1, 1, 2, 0), (3, 1, 2, 0, 3, 0), (9, 0, 3, 3, 2, 1), (15, 3, 2, 0, 5, 0), (25, 0, 5, 5, 3, 1), (40, 5, 2, 0, 8, 0))

    def f_slots(t):
        a, b = 7, 0
        for t0, a0, na, b0, nb, inner in f_rects[::-1]:
            u = t - t0
            pa, pb = (a0 + u % na, b0 + u // na) if inner else (a0 + u // nb, b0 + u % nb)
            a = jnp.where(t < T_LAST if t0 == 40 else t < t_next, pa, a)
            b = jnp.where(t < T_LAST if t0 == 40 else t < t_next, pb, b)
            t_next = t0
        return col_slot(a), jnp.where(t < T_LAST, row_slot(b), t - T_LAST)

    def f_block(t, second):
        return two_blocks(*f_slots(t), second)

    def f_scores(sc, blk):
        ks, qs, kh, qh = blk
        sc[...] = mm(k_s[ks, kh, :, 0:QK], qt_s[qs, qh])

    def f_use(sc, blk, mask=False):
        ks, qs, kh, qh = blk
        s = sc[...]
        if mask:
            keys = lax.broadcasted_iota(jnp.int32, (HALF, HALF), 0)
            rows = lax.broadcasted_iota(jnp.int32, (HALF, HALF), 1)
            s = jnp.where(keys <= rows, s, NEG_BIG)
        m0 = m_s[qs, qh]
        m1 = jnp.maximum(m0, jnp.max(s, axis=0, keepdims=True))
        p = jnp.exp2((s - m1) * EXP2_SCALE)
        alpha = jnp.exp2((m0 - m1) * EXP2_SCALE)
        l_s[qs, qh] = l_s[qs, qh] * alpha + jnp.sum(p, axis=0, keepdims=True)
        m_s[qs, qh] = m1
        ot_s[qs, qh] = ot_s[qs, qh] * alpha + mm(vt_s[ks, kh, 0:VAL], p.astype(BF))

    def own_f():
        for kh, qh in ((0, 0), (0, 1), (1, 1)):
            blk = (row, col, kh, qh)
            f_scores(sc0, blk)
            f_use(sc0, blk, mask=kh == qh)

    own_f()

    def stats_copy(slot, n):
        return pltpu.make_async_remote_copy(st_s.at[slot], st_r.at[slot, col], st_send.at[slot, n - 1], st_recv.at[slot], device_id=row_dev(n))

    def make_stats(qs):
        for h in range(2):
            d = jnp.sum(ot_s[qs, h] * dot_s[qs, h].astype(F32), axis=0, keepdims=True)
            for j in range(4):
                c = slice(128 * j, 128 * j + 128)
                r = 4 * h + j
                st_s[qs, r:r + 1] = m_s[qs, h, :, c]
                st_s[qs, 8 + r:9 + r] = l_s[qs, h, :, c]
                st_s[qs, 16 + r:17 + r] = d[:, c]

    def start_stats(qs):
        for n in range(1, 8):
            stats_copy(qs, n).start()
        st_r[qs, col] = st_s[qs]

    q_steps, q_ranks = (1, 2, 9, 12, 25, 30, 35), (1, 2, 3, 4, 5, 6, 7)
    k_steps, k_ranks = (3, 6, 15, 20, 40, 48, T_LAST), (1, 2, 3, 4, 5, 6, 7)
    do_steps, do_ranks = (49, 50, 51, 52, 53, 54), (1, 2, 3, 5, 6, 7)

    def f_arrive(t):
        @pl.when(among(t, tuple(sorted(set(q_steps + k_steps + do_steps + (T_RELAY_Q, T_RELAY_K, T_OWN_DO, T_RELAY_DO))))))
        def _():
            @pl.when(among(t, q_steps))
            def _():
                rank = at(t, q_steps, q_ranks)

                @pl.when(rank != 4)
                def _():
                    wait_q(rank)
                place_q(row_slot(rank))

            @pl.when(among(t, k_steps))
            def _():
                rank = at(t, k_steps, k_ranks)

                @pl.when(rank != 4)
                def _():
                    wait_k(rank)
                place_k(col_slot(rank))

            @pl.when(among(t, do_steps))
            def _():
                rank = at(t, do_steps, do_ranks)
                wait_do(rank)
                place_do(row_slot(rank))

            @pl.when(t == T_RELAY_Q)
            def _():
                wait_q(4)
                for n in range(3):
                    start(q_copies(4 + n, row_slot(4), row_dev(n + 1)))

            @pl.when(t == T_RELAY_K)
            def _():
                wait_k(4)
                for n in range(3):
                    start(k_copies(4 + n, col_slot(4), col_dev(n + 1)))

            @pl.when(t == T_OWN_DO)
            def _():
                for n in (3, 0, 1, 2):
                    start(do_copies(n, col, row_dev(n + 1)))

            @pl.when(t == T_RELAY_DO)
            def _():
                wait_do(4)
                for n in range(3):
                    start(do_copies(4 + n, row_slot(4), row_dev(n + 1)))
                place_do(row_slot(4))

    f_arrive(1)
    f_scores(sc0, f_block(1, False))
    f_arrive(2)

    def f_step(t, _):
        nxt = jnp.minimum(t + 1, 63)
        b1, b2 = f_block(t, False), f_block(t, True)
        f_scores(sc1, b2)
        f_use(sc0, b1)
        f_scores(sc0, f_block(nxt, False))
        f_use(sc1, b2)

        @pl.when(t >= T_LAST)
        def _():
            @pl.when(t > T_LAST)
            def _():
                start_stats(t - T_LAST - 1)

            make_stats(t - T_LAST)

        f_arrive(t + 2)
        return 0

    lax.fori_loop(1, 64, f_step, 0)
    start_stats(7)

    def ring_dev(s):
        return {'cp': 8 * row + 4 * y0 + s % 4}

    def o_copies(s):
        d = (s // 4) ^ y0
        return [pltpu.make_async_remote_copy(ot_s.at[s, h], xo.at[d, x, pl.ds(h * VAL, VAL)], xo_send.at[h, s], xo_recv.at[h, d, x], device_id=ring_dev(s)) for h in range(2)]

    def dq_refs(s, rows):
        return [dq_s.at[s, 0, rows], dq_s.at[s, 1, rows], dqr_s.at[s, rows]]

    def dq_copies(rank):
        d, n = rank // 4, rank % 4 - 1
        srcs = dq_refs(row_slot(rank), pl.ds(0, HALF))
        return [pltpu.make_async_remote_copy(srcs[j], xq.at[d, n, :, pl.ds(128 * j, 128)], xq_send.at[j, rank], xq_recv.at[j, d, n], device_id=row_dev(n + 1)) for j in range(3)]

    def dq_via(d, p):
        srcs = dq_refs(row_slot(4 * d + 3), pl.ds(p * (HALF // 2), HALF // 2))
        return [pltpu.make_async_remote_copy(srcs[j], xqv.at[d, p, :, pl.ds(128 * j, 128)], xqv_send.at[j, d, p], xqv_recv.at[j, d, p], device_id=row_dev(p + 1)) for j in range(3)]

    def dkv_copies(rank):
        d, n = rank // 4, rank % 4 - 1
        s = col_slot(rank)
        out = []
        for h in range(2):
            out.append(pltpu.make_async_remote_copy(dk_s.at[s, h], zkv.at[d, n, h, pl.ds(0, QK)], zkv_send.at[0, h, rank], zkv_recv.at[0, h, d, n], device_id=col_dev(n + 1)))
            out.append(pltpu.make_async_remote_copy(dv_s.at[s, h], zkv.at[d, n, h, pl.ds(QK, VAL)], zkv_send.at[1, h, rank], zkv_recv.at[1, h, d, n], device_id=col_dev(n + 1)))
        return out

    def dkv_via(d, h):
        s = col_slot(4 * d + 3)
        return [
            pltpu.make_async_remote_copy(dk_s.at[s, h], zkvv.at[d, h, pl.ds(0, QK)], zkvv_send.at[0, d, h], zkvv_recv.at[0, d, h], device_id=col_dev(h + 1)),
            pltpu.make_async_remote_copy(dv_s.at[s, h], zkvv.at[d, h, pl.ds(QK, VAL)], zkvv_send.at[1, d, h], zkvv_recv.at[1, d, h], device_id=col_dev(h + 1)),
        ]

    def o_wait(d, r):
        s = (x + gray(r)) % 4
        for h in range(2):
            pltpu.make_async_remote_copy(ot_s.at[0, h], xo.at[d, s, pl.ds(h * VAL, VAL)], xo_send.at[h, r], xo_recv.at[h, d, s], device_id=row_dev(r)).wait_recv()

    def local(pairs):
        return [pltpu.make_async_copy(src, dst, loc.at[n]) for n, (src, dst) in enumerate(pairs)]

    def done(copies):
        for c in copies:
            c.wait()

    def rows(n, size):
        return stg.at[pl.ds(n, size)]

    pair_row = row_dev(4)
    pair_col = col_dev(4)

    def o_pair():
        s = row_slot(4)
        return [pltpu.make_async_remote_copy(ot_s.at[s, h], po.at[pl.ds(h * VAL, VAL)], p_send.at[h], p_recv.at[h], device_id=pair_row) for h in range(2)]

    def dq_pair():
        s = row_slot(4)
        srcs = dq_refs(s, pl.ds(0, HALF))
        return [pltpu.make_async_remote_copy(srcs[j], pq.at[:, pl.ds(128 * j, 128)], p_send.at[2 + j], p_recv.at[2 + j], device_id=pair_row) for j in range(3)]

    def dkv_pair():
        s = col_slot(4)
        out = []
        for h in range(2):
            out.append(pltpu.make_async_remote_copy(dk_s.at[s, h], pkv.at[h, pl.ds(0, QK)], p_send.at[5 + 2 * h], p_recv.at[5 + 2 * h], device_id=pair_col))
            out.append(pltpu.make_async_remote_copy(dv_s.at[s, h], pkv.at[h, pl.ds(QK, VAL)], p_send.at[6 + 2 * h], p_recv.at[6 + 2 * h], device_id=pair_col))
        return out

    KV = QK + VAL

    def o_local(d):
        return local([(xo.at[d, (x + gray(r)) % 4], rows(2 * VAL * (r - 1), 2 * VAL)) for r in range(1, 4)])

    def fetch_o(d):
        for r in range(1, 4):
            o_wait(d, r)
        start(o_local(d))

    def add_o(slot, d):
        done(o_local(d))
        for h in range(2):
            a, b, c = (stg[2 * VAL * n + h * VAL:2 * VAL * n + (h + 1) * VAL] for n in range(3))
            ot_s[slot, h] = ot_s[slot, h] + (a + b + c)

    def dkv_local(d):
        return local([(zkv.at[d, n, h], rows(KV * (2 * h + n), KV)) for h in range(2) for n in range(2)])

    def fetch_dkv(d):
        for c in dkv_copies(4 * d + 1) + dkv_copies(4 * d + 2):
            c.wait_recv()
        start(dkv_local(d))

    def add_dkv(slot, d):
        done(dkv_local(d))
        for h in range(2):
            a, b = KV * 2 * h, KV * (2 * h + 1)
            dk_s[slot, h] = dk_s[slot, h] + (stg[a:a + QK] + stg[b:b + QK])
            dv_s[slot, h] = dv_s[slot, h] + (stg[a + QK:a + KV] + stg[b + QK:b + KV])

    def via_local(d, h):
        return local([(zkvv.at[d, h], rows(0, KV))])

    def fetch_via(d, h):
        for c in dkv_via(d, h):
            c.wait_recv()
        start(via_local(d, h))

    def add_via(d, h):
        done(via_local(d, h))
        slot = col_slot(4 * d + 1 + h)
        dk_s[slot, h] = dk_s[slot, h] + stg[0:QK]
        dv_s[slot, h] = dv_s[slot, h] + stg[QK:KV]

    def add_dq_via(d):
        for p in range(2):
            for c in dq_via(d, p):
                c.wait_recv()
        copies = local([(xqv.at[d, p], stg.at[pl.ds(p * HALF, HALF // 2), pl.ds(0, 384)]) for p in range(2)])
        start(copies)
        done(copies)
        for p in range(2):
            slot = row_slot(4 * d + 1 + p)
            r = slice(p * (HALF // 2), (p + 1) * (HALF // 2))
            u = slice(p * HALF, p * HALF + HALF // 2)
            for j in range(2):
                dq_s[slot, j, r] = dq_s[slot, j, r] + stg[u, 128 * j:128 * j + 128]
            dqr_s[slot, r] = dqr_s[slot, r] + stg[u, 256:384]

    def dq_local(d):
        return local([(xq.at[d, n], stg.at[pl.ds(n * HALF, HALF), pl.ds(0, 384)]) for n in range(2)])

    def sum_dq(slot, d):
        for c in dq_copies(4 * d + 1) + dq_copies(4 * d + 2):
            c.wait_recv()
        start(dq_local(d))
        done(dq_local(d))
        for j in range(2):
            c = slice(128 * j, 128 * j + 128)
            dq_s[slot, j] = dq_s[slot, j] + (stg[0:HALF, c] + stg[HALF:2 * HALF, c])
        dqr_s[slot] = dqr_s[slot] + (stg[0:HALF, 256:384] + stg[HALF:2 * HALF, 256:384])

    def columns(v):
        flat = jnp.concatenate([v[j:j + 1] for j in range(4)], axis=1)
        hi = flat.astype(BF).astype(F32)
        mid = (flat - hi).astype(BF).astype(F32)
        lo = flat - hi - mid
        return jnp.concatenate([hi, mid, lo, jnp.zeros((AUG - 3, HALF), F32)], axis=0).T.astype(BF)

    def wait_stats(qs):
        pltpu.make_async_copy(st_r.at[qs, pl.ds(0, 7)], st_r.at[qs, pl.ds(0, 7)], st_recv.at[qs]).wait()

    def prepare(qs):
        wait_stats(qs)
        m = st_r[qs, :, 0:8]
        m_all = jnp.max(m, axis=0)
        w = jnp.exp2((m - m_all[None]) * EXP2_SCALE)
        l_all = jnp.sum(w * st_r[qs, :, 8:16], axis=0)
        inv = 1.0 / l_all
        delta = jnp.sum(w * st_r[qs, :, 16:24], axis=0) * inv
        lse = m_all + jnp.log2(l_all) * (1.0 / EXP2_SCALE)
        mine = jnp.exp2((st_s[qs, 0:8] - m_all) * EXP2_SCALE) * inv
        for h in range(2):
            q_s[qs, h, :, QK:QK + AUG] = columns(-lse[4 * h:4 * h + 4])
            do_s[qs, h, :, VAL:VAL + AUG] = columns(-delta[4 * h:4 * h + 4])
            for j in range(4):
                r = 4 * h + j
                c = slice(128 * j, 128 * j + 128)
                ot_s[qs, h, :, c] = ot_s[qs, h, :, c] * mine[r:r + 1]

    k_first, q_last = (7, 3, 5, 6, 4, 1, 2), (7, 5, 6, 3, 1, 2, 4)

    def b_slots(t):
        a = jnp.where(t < 56, order(t // 8, k_first), 0)
        return col_slot(a), jnp.where(t < 56, t % 8, row_slot(order(t - 56, q_last)))

    def b_block(t, second):
        return two_blocks(*b_slots(t), second)

    def b_scores(sc, dp, blk):
        ks, qs, kh, qh = blk
        sc[...] = mm(q_s[qs, qh], kt_s[ks, kh])
        dp[...] = mm(do_s[qs, qh], vt_s[ks, kh])

    def b_elem(sc, dp, pr, ds, blk, mask=False):
        p = jnp.exp2(sc[...] * EXP2_SCALE)
        if mask:
            rows = lax.broadcasted_iota(jnp.int32, (HALF, HALF), 0)
            keys = lax.broadcasted_iota(jnp.int32, (HALF, HALF), 1)
            p = jnp.where(keys <= rows, p, 0.0)
        pr[...] = p.astype(BF)
        ds[...] = (p * dp[...]).astype(BF)

    def b_grads(pr, ds, blk):
        ks, qs, kh, qh = blk
        p = pr[...]
        g = ds[...]
        dv_s[ks, kh] += mm(dot_s[qs, qh], p)
        dk_s[ks, kh] += mm(qt_s[qs, qh], g)
        dq = mm(g, k_s[ks, kh])
        dq_s[qs, qh] += dq[:, 0:NOPE]
        side = lax.broadcasted_iota(jnp.int32, (1, 128), 1) // ROPE
        dqr_s[qs] += jnp.where(side == qh, dq[:, NOPE:], 0.0)

    pr1[...] = jnp.zeros((HALF, HALF), BF)
    ds1[...] = jnp.zeros((HALF, HALF), BF)
    prepare(0)
    prepare(1)
    b_scores(sc0, dp0, b_block(0, False))

    fetch_steps, add_steps, send_steps = (24, 32, 48, 56), (25, 33, 49, 57), (26, 34, 50, 58)

    def b_events(t):
        @pl.when((t < 9) | among(t, (9, 17, T_PAIR_O - 1, T_PAIR_O, T_PAIR_O + 1, T_PAIR_KV - 1, T_PAIR_KV, T_PAIR_KV + 1, 61) + fetch_steps + add_steps + send_steps))
        def _():
            @pl.when(t < 7)
            def _():
                prepare(t + 1)

            @pl.when((t < 9) & ((t - 1) % 4 != x))
            def _():
                start(o_copies(t - 1))

            @pl.when((t == 9) | (t == 17))
            def _():
                for h in range(2):
                    start(dkv_via(jnp.where(t == 9, 1, 0), h))

            @pl.when(among(t, fetch_steps))
            def _():
                fetch_via(jnp.where(t < 40, 1, 0), jnp.where(among(t, fetch_steps[1::2]), 1, 0))

            @pl.when(among(t, add_steps))
            def _():
                add_via(jnp.where(t < 40, 1, 0), jnp.where(among(t, add_steps[1::2]), 1, 0))

            @pl.when(among(t, send_steps))
            def _():
                start(dkv_copies(at(t, send_steps, (5, 6, 1, 2))))

            @pl.when(t == 58)
            def _():
                for p in range(2):
                    start(dq_via(1, p))

            @pl.when(t == 61)
            def _():
                for p in range(2):
                    start(dq_via(0, p))

            @pl.when(t == T_PAIR_O - 1)
            def _():
                fetch_o(1)

            @pl.when(t == T_PAIR_O)
            def _():
                add_o(row_slot(4), 1)

            @pl.when(t == T_PAIR_O + 1)
            def _():
                start(o_pair())

            @pl.when(t == T_PAIR_KV - 1)
            def _():
                fetch_dkv(1)

            @pl.when(t == T_PAIR_KV)
            def _():
                add_dkv(col_slot(4), 1)

            @pl.when(t == T_PAIR_KV + 1)
            def _():
                start(dkv_pair())

    def b_step(t, _):
        b1, b2 = b_block(t, False), b_block(t, True)
        prev = b_block(jnp.maximum(t - 1, 0), True)
        nxt = b_block(jnp.minimum(t + 1, 62), False)
        b_scores(sc1, dp1, b2)
        b_elem(sc0, dp0, pr0, ds0, b1)
        b_grads(pr1, ds1, prev)
        b_scores(sc0, dp0, nxt)
        b_elem(sc1, dp1, pr1, ds1, b2)
        b_grads(pr0, ds0, b1)
        b_events(t + 1)
        return 0

    lax.fori_loop(0, 63, b_step, 0)
    b_grads(pr1, ds1, b_block(62, True))

    def own_b():
        for kh, qh in ((0, 0), (0, 1), (1, 1)):
            blk = (row, col, kh, qh)
            b_scores(sc0, dp0, blk)
            b_elem(sc0, dp0, pr0, ds0, blk, mask=kh == qh)
            b_grads(pr0, ds0, blk)

    fetch_o(0)
    own_b()

    def finish_o():
        add_o(col, 0)
        for c in o_pair():
            c.wait_recv()
        last_o = local([(po, sc0.at[pl.ds(0, 2 * VAL)])])
        start(last_o)
        for n in range(4):
            for c in do_copies(n, col, row_dev(n + 1)):
                c.wait_send()
        done(last_o)
        for h in range(2):
            do_s[col, h, :, 0:VAL] = (ot_s[col, h] + sc0[h * VAL:(h + 1) * VAL]).T.astype(BF)
        return pltpu.make_async_copy(do_s.at[col, :, :, pl.ds(0, VAL)], out_o, outs.at[0])

    o_out = finish_o()
    o_out.start()
    add_dq_via(1)
    for h in range(2):
        (pr0, pr1)[h][...] = c_in[h].T
    start(dq_copies(5))
    start(dq_copies(6))
    add_dq_via(0)
    w_all = jnp.concatenate([wk_in[...], wv_in[...]], axis=1).astype(F32)
    start(dq_copies(1))
    start(dq_copies(2))

    def finish_dkv():
        fetch_dkv(0)
        for c in dkv_pair():
            c.wait_recv()
        pairs = [pltpu.make_async_copy(pkv.at[h], (sc0, sc1)[h].at[pl.ds(0, KV)], loc.at[4 + h]) for h in range(2)]
        start(pairs)
        done(dkv_local(0))
        done(pairs)
        sums = None
        for h in range(2):
            a, b, other = KV * 2 * h, KV * (2 * h + 1), (sc0, sc1)[h]
            dk = (dk_s[row, h] + (stg[a:a + QK] + stg[b:b + QK]) + other[0:QK]) * SCALE
            dv = dv_s[row, h] + (stg[a + QK:a + KV] + stg[b + QK:b + KV]) + other[QK:KV]
            rope_s[:, h * HALF:(h + 1) * HALF] = dk[NOPE:QK]
            kv = jnp.concatenate([dk[0:NOPE].T, dv.T], axis=1)
            part = mm((pr0, pr1)[h][...].astype(F32), kv)
            sums = part if h == 0 else sums + part
            stg[2 * h * HALF:2 * h * HALF + HALF, 0:2 * NOPE] = kv
        w_s[0] = sums[:, 0:NOPE]
        w_s[1] = sums[:, NOPE:]

    finish_dkv()

    def w_copy(src, dst, n, m, dev):
        return pltpu.make_async_remote_copy(src, dst, w_send.at[n], w_recv.at[m], device_id=dev)

    mate = {'data': 1 - core}
    first = w_copy(w_s.at[1 - core], ws_r, 0, 0, mate)
    first.start()

    def finish_c():
        for h in range(2):
            (dp0, dp1)[h][...] = mm_t(stg[2 * h * HALF:2 * h * HALF + HALF, 0:2 * NOPE], w_all)

    finish_c()
    c_out = [pltpu.make_async_copy(dp0, out_c.at[0], outs.at[1]), pltpu.make_async_copy(dp1, out_c.at[1], outs.at[2])]
    r_out = [pltpu.make_async_copy(rope_s, out_r, outs.at[3])]
    start(c_out)
    start(r_out)

    def w_one():
        first.wait_recv()
        wr_s[...] = w_s[core] + ws_r[...]

    w_one()

    def along_col(r):
        s = col_slot(r)
        return pltpu.make_async_remote_copy(wr_s.at[pl.ds(64 * s, 64)], wr_r.at[row], w_send.at[r], w_recv.at[1], device_id=col_dev(r))

    for r in range(1, 8):
        along_col(r).start()
    strip = pl.ds(pl.multiple_of(64 * row, 64), 64)
    wr_r[row] = wr_s[strip]

    def finish_dq_pair():
        sum_dq(row_slot(4), 1)

    finish_dq_pair()

    def w_two():
        pltpu.make_async_copy(wr_r.at[pl.ds(0, 7)], wr_r.at[pl.ds(0, 7)], w_recv.at[1]).wait()
        wc_s[...] = jnp.sum(wr_r[...], axis=0)

    start(dq_pair())
    w_two()

    def along_row(r):
        return pltpu.make_async_remote_copy(wc_s, wc_r.at[col], w_send.at[7 + r], w_recv.at[2], device_id=row_dev(r))

    for r in range(1, 8):
        along_row(r).start()
    wc_r[col] = wc_s[...]

    def w_three():
        pltpu.make_async_copy(wc_r.at[pl.ds(0, 7)], wc_r.at[pl.ds(0, 7)], w_recv.at[2]).wait()
        w_s[core, strip] = jnp.sum(wc_r[...], axis=0)

    w_three()

    def back_col(r):
        return pltpu.make_async_remote_copy(w_s.at[core, strip], w_s.at[core, strip], w_send.at[14 + r], w_recv.at[3], device_id=col_dev(r))

    for r in range(1, 8):
        back_col(r).start()

    def finish_dq():
        for c in dq_copies(1) + dq_copies(2):
            c.wait_recv()
        for c in dq_pair():
            c.wait_recv()
        copies = local([(xq.at[0, 0], stg.at[pl.ds(0, HALF), pl.ds(0, 384)]), (xq.at[0, 1], stg.at[pl.ds(HALF, HALF), pl.ds(0, 384)]), (pq, stg.at[pl.ds(2 * HALF, HALF), pl.ds(0, 384)])])
        start(copies)
        done(copies)

        def total(mine, c):
            return (mine + (stg[0:HALF, c] + stg[HALF:2 * HALF, c]) + stg[2 * HALF:3 * HALF, c]) * SCALE

        for h in range(2):
            q_out_s[0:NOPE, h * HALF:(h + 1) * HALF] = total(dq_s[col, h], slice(128 * h, 128 * h + 128)).T
        rope = total(dqr_s[col], slice(256, 384)).T
        for h in range(2):
            q_out_s[NOPE:QK, h * HALF:(h + 1) * HALF] = rope[h * ROPE:(h + 1) * ROPE]
        return pltpu.make_async_copy(q_out_s, out_q, outs.at[5])

    def w_four():
        first.wait_send()
        pltpu.make_async_copy(wr_s.at[pl.ds(0, 448)], wr_s.at[pl.ds(0, 448)], w_recv.at[3]).wait()

    w_four()
    last = w_copy(w_s.at[core], wl_r, 22, 4, mate)
    last.start()
    q_out = finish_dq()
    q_out.start()

    def w_five():
        last.wait_recv()
        w_s[1 - core] = wl_r[...]

    w_five()
    w_out = [pltpu.make_async_copy(w_s.at[0], out_uk, outs.at[6]), pltpu.make_async_copy(w_s.at[1], out_uv, outs.at[7])]
    start(w_out)

    last.wait_send()
    for r in range(1, 8):
        along_row(r).wait_send()
        along_col(r).wait_send()
        back_col(r).wait_send()
        for s in range(8):
            stats_copy(s, r).wait_send()
        if r != 4:
            for c in o_copies(row_slot(r)):
                c.wait_send()
        if r % 4 in (1, 2):
            for c in dkv_copies(r) + dq_copies(r):
                c.wait_send()
        if r % 4 == 3:
            for h in range(2):
                for c in dkv_via(r // 4, h) + dq_via(r // 4, h):
                    c.wait_send()
    for c in o_pair() + dkv_pair() + dq_pair():
        c.wait_send()
    for n in range(4):
        for c in q_copies(n, col, row_dev(n + 1)) + k_copies(n, row, col_dev(n + 1)):
            c.wait_send()
    for n in range(3):
        for c in q_copies(4 + n, row_slot(4), row_dev(n + 1)) + k_copies(4 + n, col_slot(4), col_dev(n + 1)) + do_copies(4 + n, row_slot(4), row_dev(n + 1)):
            c.wait_send()
    for c in [o_out, q_out] + c_out + r_out + w_out:
        c.wait()


def core_call(c, kpe, q, wk, wv, do):
    vmem = pltpu.VMEM
    dma = pltpu.SemaphoreType.DMA
    n = 8
    shape = jax.ShapeDtypeStruct
    scratch = [
        vmem((n, 2, HALF, QK + AUG), BF), vmem((n, HALF, 128), BF), vmem((n, 2, HALF, QK + ROPE), BF), vmem((n, HALF, 128), BF),
        vmem((n, 2, VAL + AUG, HALF), BF), vmem((n, 2, HALF, VAL + AUG), BF),
        vmem((n, 2, QK, HALF), BF), vmem((n, 2, QK + AUG, HALF), BF), vmem((n, 2, VAL, HALF), BF),
        vmem((n, 2, VAL, HALF), F32), vmem((n, 2, 1, HALF), F32), vmem((n, 2, 1, HALF), F32),
        vmem((n, 2, HALF, NOPE), F32), vmem((n, HALF, 128), F32), vmem((n, 2, QK, HALF), F32), vmem((n, 2, VAL, HALF), F32),
        vmem((n, 24, 128), F32), vmem((n, n, 24, 128), F32), vmem((3 * HALF, HALF), F32),
        vmem((2, LATENT, 128), F32), vmem((LATENT, 128), F32), vmem((LATENT, 128), F32), vmem((ROPE, 2 * HALF), F32), vmem((QK, 2 * HALF), F32), vmem((LATENT, 128), F32), vmem((n, 64, 128), F32), vmem((64, 128), F32), vmem((n, 64, 128), F32),
        vmem((HALF, HALF), F32), vmem((HALF, HALF), F32), vmem((HALF, HALF), F32), vmem((HALF, HALF), F32),
        vmem((HALF, HALF), BF), vmem((HALF, HALF), BF), vmem((HALF, HALF), BF), vmem((HALF, HALF), BF),
        dma((2, 7)), dma((2, n)), dma((3, 7)), dma((3, n)), dma((7,)), dma((n,)), dma((n, 7)), dma((n,)),
        dma((2, n)), dma((2, 2, 4)), dma((3, n)), dma((3, 2, 2)), dma((3, 2, 2)), dma((3, 2, 2)), dma((2, 2, n)), dma((2, 2, 2, 2)), dma((2, 2, 2)), dma((2, 2, 2)), dma((9,)), dma((9,)), dma((6,)), dma((8,)),
        dma((23,)), dma((5,)),
    ]
    outs = (
        shape((2, HALF, VAL), BF), shape((QK, 2 * HALF), F32), shape((2, HALF, LATENT), F32), shape((ROPE, 2 * HALF), F32),
        shape((LATENT, NOPE), F32), shape((LATENT, VAL), F32),
        shape((2, 4, 2 * VAL, HALF), F32), shape((2, 2, HALF, 384), F32), shape((2, 2, HALF // 2, 384), F32),
        shape((2, 2, 2, QK + VAL, HALF), F32), shape((2, 2, QK + VAL, HALF), F32),
        shape((2 * VAL, HALF), F32), shape((HALF, 384), F32), shape((2, QK + VAL, HALF), F32),
    )
    return pl.pallas_call(
        core_kernel,
        out_shape=outs,
        in_specs=[pl.BlockSpec(memory_space=pltpu.VMEM)] * 6,
        out_specs=[pl.BlockSpec(memory_space=pl.ANY)] * len(outs),
        scratch_shapes=scratch,
        compiler_params=pltpu.CompilerParams(collective_id=0, has_side_effects=True, vmem_limit_bytes=67043328),
        name='core',
    )(c, kpe, q, wk, wv, do)[:6]


def solution(mesh):
    token_spec = P(('pod', 'data'), 'cp', None)
    head_spec = P(('pod', 'data'), 'cp', None, None)
    weight_spec = P(None, None, None)
    sum_spec = P('pod', None, None)

    def per_device(c_latent, k_rope, queries, w_uk, w_uv, d_out):
        halves = lambda a, width: a.reshape(2, HALF, width)
        o, gq, gc, gr, guk, guv = core_call(halves(c_latent, LATENT), k_rope[0].T, queries[0, :, 0].T, w_uk[:, 0], w_uv[:, 0], halves(d_out, VAL))
        return (o.reshape(1, 2 * HALF, 1, VAL), gq.T.reshape(1, 2 * HALF, 1, QK), gc.reshape(1, 2 * HALF, LATENT),
                gr.T.reshape(1, 2 * HALF, ROPE), guk[:, None], guv[:, None])

    return jax.shard_map(per_device, mesh=mesh, in_specs=(token_spec, token_spec, head_spec, weight_spec, weight_spec, head_spec), out_specs=(head_spec, head_spec, token_spec, token_spec, sum_spec, sum_spec), check_vma=False)
```

time: 526 us -> 261 us (0.50)
  waiting for transfers between devices: 129 us -> 0 us
  Pallas kernels: 346 us -> 250 us
  other arithmetic: 16.2 us -> 0 us
  between operations: 14.2 us -> 0.66 us
  local copies, waits for them, and re-layouts: 14 us -> 7.39 us
  matrix products: 6.58 us -> 0 us
    psum x1 -> x0, waiting for transfers between devices: 129 us -> none  [per_device(): lax.psum(jnp.einsum('htl,hdt->ld', lat, dkn, preferred_element_type=F32),...]
    pallas_call x1, Pallas kernels: 346 us -> 250 us  [core_call(): pl.pallas_call(core_kernel, out_shape=outs, in_specs=[pl.BlockSpec(memory...]
    reduce_sum x4 -> x0, other arithmetic: 13 us -> none  [the longest x1 3.58 us: per_device(): dk = jnp.sum(dk_parts, axis=0) * SCALE]
    dot_general x6 -> x0, matrix products: 6.58 us -> none  [the longest x1 1.77 us: per_device(): jnp.einsum('hdt,ld->htl', dv, wv, preferred_element_type=F32)]
  transfers between devices with their start and end apart: 1 -> 0, of which waited for: 1 -> 0; matrix products, arithmetic and copies ran while one was open for 3% -> 0% of each run, Pallas kernels for 0% -> 0%
where the time goes in v2:
time: 261 us; the launch traced here: 258 us
  Pallas kernels  250 us (96%)
  local copies, waits for them, and re-layouts  7.39 us (3%)
    pallas_call x1, Pallas kernels, core_call(): pl.pallas_call(core_kernel, out_shape=outs, in_specs=[pl.BlockSpec(memory...  250 us
    unnamed x14, local copies, waits for them, and re-layouts  7.39 us

profile of v2, /device:TPU:1, one launch (start us, length us, event | category | flops | bytes accessed | tf_op | source)
XLA Modules:
  0.0 258.3 jit_solution(9113468047512908726)
XLA Ops:
  0.6 250.3 %core.1 = (bf16[2,512,128]{2,1,0:T(8,128)(2,1)}, f32[192,1024]{1,0:T(8,128)}, f32[2,512,512]{2,1,0:T(8,128)}, f32[64,1024]{1,0:T(8,128)}, f32[512,128]{1,0:T(8,1...) custom-call(bf16[2,512,512]{2,1,0:T(8,128)(2,1)} %bitcast.25, ...), custom_call_target="tpu_custom_call" | custom-call | tf_op jit(solution)/shard_map/core/pallas_call | solution.py:836
  250.9 0.0 copy-start
  250.9 1.8 copy.20
  252.8 0.0 copy-start.3
  252.8 2.1 copy.21
  254.9 0.0 copy-done
  254.9 0.0 copy-start.2
  254.9 0.0 copy-start.1
  254.9 1.3 copy.22
  256.2 0.0 copy-done.3
  256.2 0.7 copy.23
  256.9 0.0 copy-done.2
  256.9 0.7 copy.24
  257.6 0.0 copy-done.1
  257.6 0.7 copy.25
Async XLA Ops:
  250.9 4.0 %copy-start = (f32[2,512,512]{2,1,0:T(8,128)S(1)}, f32[2,512,512]{2,1,0:T(8,128)}, u32[]{:S(2)}) copy-start(f32[2,512,512]{2,1,0:T(8,128)} %get-tuple-element.14) | copy-start | bytes 6291460
  252.8 3.5 %copy-start.3 = (f32[64,1024]{1,0:T(8,128)S(1)}, f32[64,1024]{1,0:T(8,128)}, u32[]{:S(2)}) copy-start(f32[64,1024]{1,0:T(8,128)} %get-tuple-element.15) | copy-start | bytes 786436
  254.9 2.0 copy-start.2
  254.9 2.7 %copy-start.1 = (f32[512,128]{1,0:T(8,128)S(1)}, f32[512,128]{1,0:T(8,128)}, u32[]{:S(2)}) copy-start(f32[512,128]{1,0:T(8,128)} %get-tuple-element.17) | copy-start | bytes 786436

commit v3 on v0

v3 whole, which is shorter than its diff:
```python
import jax
import jax.numpy as jnp
from jax import lax
from jax.experimental import pallas as pl
from jax.experimental.pallas import tpu as pltpu
from jax.sharding import PartitionSpec as P

BF = jnp.bfloat16
F32 = jnp.float32
NEG_BIG = -1.0e30
HALF = 512
LATENT = 512
LANES = 128
NOPE = 128
ROPE = 64
QK = NOPE + ROPE
VAL = 128
KV = QK + VAL
AUG = 16
SCALE = QK ** -0.5
EXP2_SCALE = SCALE * 1.4426950408889634
TWO = 2
RING = 4
FAR = RING - 1
GROUP = 8
HALVES = range(TWO)
NEIGHBOURS = (1, 2)
PEERS = range(1, GROUP)
CHIPS = GROUP * GROUP
STRIP = LATENT // CHIPS
ROWS = HALF // TWO
BLOCKS = HALF // LANES
Q_STEPS = (1, 2, 9, 12, 25, 30, 35)
K_STEPS = (3, 6, 15, 20, 40, 48, 56)
DO_STEPS, DO_RANKS = (49, 50, 51, 52, 53, 54), (1, 2, 3, 5, 6, 7)
T_RELAY, T_OWN_DO, T_RELAY_DO = 9, 12, 34
T_LAST = 56
T_END = 64
RECTS = ((1, 0, 1, 1, 2, False), (3, 1, 2, 0, 3, False), (9, 0, 3, 3, 2, True), (15, 3, 2, 0, 5, False), (25, 0, 5, 5, 3, True), (40, 5, 2, 0, 8, False))
K_ORDER = (7, 3, 5, 6, 4, 1, 2)
Q_ORDER = (7, 5, 6, 3, 1, 2, 4)
T_SPLIT, T_OWN = 48, 56
T_VIA = (9, 17)
T_FETCH, T_ADD = (21, 31), (22, 32)
T_NEAR, NEAR = (25, 33, 49), (5, 6, 1)
T_NEAR_MID, T_NEAR_LAST = 53, 57
T_PAIR_O = 38
T_PAIR_KV = (46, 54)
T_VIA_Q, T_Q_FIVE, T_Q_SIX = 58, 59, 60


def mm(a, b):
    return jnp.dot(a, b, preferred_element_type=F32)


def mm_t(a, b):
    return lax.dot_general(a, b, (((1,), (1,)), ((), ())), preferred_element_type=F32)


def gray(r):
    return r ^ (r >> 1)


def part(n, size):
    return slice(n * size, (n + 1) * size)


def rows_of(n, size):
    return pl.ds(pl.multiple_of(n * size, size), size)


def order(n, ranks):
    out = ranks[-1]
    for i, r in list(enumerate(ranks))[-2::-1]:
        out = jnp.where(n <= i, r, out)
    return out


def among(t, steps):
    out = t == steps[0]
    for v in steps[1:]:
        out = out | (t == v)
    return out


def at(t, steps, ranks):
    out = ranks[-1]
    for v, r in list(zip(steps, ranks))[-2::-1]:
        out = jnp.where(t <= v, r, out)
    return out


def start(copies):
    for c in copies:
        c.start()


def done(copies):
    for c in copies:
        c.wait()


def landed(copies):
    for c in copies:
        c.wait_recv()


def left(copies):
    for c in copies:
        c.wait_send()


def remote(pairs, send, recv, dev):
    return [pltpu.make_async_remote_copy(src, dst, send.at[n], recv.at[n], device_id=dev) for n, (src, dst) in enumerate(pairs)]


def ring_sums(slot, dev, srcs, dsts, bufs, sems):
    main, via, pair = bufs
    main_send, main_recv, via_send, via_recv, pair_send, pair_recv = sems

    def near(rank, p):
        d, n = rank // RING, rank % RING - 1
        return remote(zip(srcs(slot(rank), p), dsts(main.at[d, n, p])), main_send.at[rank, p], main_recv.at[d, n, p], dev(n + 1))

    def far(d, p):
        return remote(zip(srcs(slot(RING * d + FAR), p), dsts(via.at[d, p])), via_send.at[d, p], via_recv.at[d, p], dev(p + 1))

    def across(p):
        return remote(zip(srcs(slot(RING), p), dsts(pair.at[p])), pair_send.at[p], pair_recv.at[p], dev(RING))

    return near, far, across


def core_kernel(c_in, kpe_in, q_in, wk_in, wv_in, do_in,
                out_o, out_q, out_c, out_r, out_uk, out_uv, xo, po, xq, xqv, pq, zkv, zkvv, pkv,
                q_s, qr_s, k_s, kr_s, vt_s, do_s, qt_s, kt_s, dot_s,
                ot_s, m_s, l_s, dq_s, dqr_s, dk_s, dv_s, st_s, st_r, stg, w_s, ws_r, wl_r, rope_s, q_out_s, wr_s, wr_r,
                sc0, sc1, dp0, dp1, pr0, pr1, ds0, ds1,
                q_send, q_recv, k_send, k_recv, do_send, do_recv, st_send, st_recv, xo_send, xo_recv, po_send, po_recv,
                q_sums_sems, kv_sums_sems, loc, outs, w_send, w_recv, strip_send, strip_recv):
    me = lax.axis_index('cp')
    core = lax.axis_index('data')
    row, col = me // GROUP, me % GROUP
    x, y0 = col % RING, col // RING
    y1, z = row % TWO, row // TWO

    def row_slot(rank):
        return RING * (y0 ^ (rank // RING)) + (x + gray(rank % RING)) % RING

    def col_slot(rank):
        return TWO * ((z + gray(rank % RING)) % RING) + (y1 ^ (rank // RING))

    def row_dev(rank):
        return {'cp': GROUP * row + row_slot(rank)}

    def col_dev(rank):
        return {'cp': GROUP * col_slot(rank) + col}

    mate = {'data': 1 - core}
    barrier = pltpu.get_barrier_semaphore()

    def to_others(act):
        def one(n, carry):
            act((me + n) % CHIPS)
            return carry

        lax.fori_loop(1, CHIPS, one, 0)

    to_others(lambda d: pl.semaphore_signal(barrier, inc=1, device_id={'cp': d}))
    pl.semaphore_signal(barrier, inc=1, device_id=mate)

    wvt = wv_in[:].T
    for h in HALVES:
        q = q_in[:, part(h, HALF)]
        qt_s[col, h] = q
        q_s[col, h, :, :QK] = q.T
        qr_s[col, :, part(h, ROPE)] = q[NOPE:].T
        do_s[col, h, :, :VAL] = do_in[h]
    for h in HALVES:
        k_s[row, h, :, :NOPE] = mm(c_in[h], wk_in[:]).astype(BF)
        rope = kpe_in[:, part(h, HALF)].T
        k_s[row, h, :, NOPE:] = jnp.concatenate([rope, rope], axis=1)
        kr_s[row, :, part(h, ROPE)] = rope
        vt_s[row, h, :VAL] = mm_t(wvt, c_in[h]).astype(BF)

    pl.semaphore_wait(barrier, CHIPS)

    def q_copies(n, slot, dev):
        refs = [q_s.at[slot, :, :, :NOPE], qr_s.at[slot]]
        return remote(zip(refs, refs), q_send.at[n], q_recv.at[slot], dev)

    def k_copies(n, slot, dev):
        refs = [k_s.at[slot, :, :, :NOPE], kr_s.at[slot], vt_s.at[slot, :, :VAL]]
        return remote(zip(refs, refs), k_send.at[n], k_recv.at[slot], dev)

    def do_copies(n, slot, dev):
        ref = do_s.at[slot, :, :, :VAL]
        return remote([(ref, ref)], do_send.at[n], do_recv.at[slot], dev)

    first_copies = (FAR, *range(FAR))

    def own_copies(copies, slot, dev, n):
        return copies(n, slot(0), dev(n + 1))

    def pair_copies(copies, slot, dev, n):
        return copies(RING + n, slot(RING), dev(n + 1))

    q_kind, k_kind, do_kind = (q_copies, row_slot, row_dev), (k_copies, col_slot, col_dev), (do_copies, row_slot, row_dev)

    for n in first_copies:
        start(own_copies(*q_kind, n))
        start(own_copies(*k_kind, n))

    def arrived(copies, slot, dev, rank):
        landed(copies(0, slot(rank), dev(1)))

    def wait_q(rank):
        arrived(*q_kind, rank)

    def wait_k(rank):
        arrived(*k_kind, rank)

    def wait_do(rank):
        arrived(*do_kind, rank)

    ones = jnp.where(lax.broadcasted_iota(jnp.int32, (AUG, HALF), 0) < 3, 1.0, 0.0).astype(BF)

    def clear(s, carry):
        for h in HALVES:
            for ref in (ot_s, dq_s, dk_s, dv_s, l_s):
                ref[s, h] = jnp.zeros(ref.shape[TWO:], F32)
            m_s[s, h] = jnp.full(m_s.shape[TWO:], NEG_BIG, F32)
            kt_s[s, h, QK:] = ones
            vt_s[s, h, VAL:] = ones
        dqr_s[s] = jnp.zeros((HALF, LANES), F32)
        return carry

    def place_q(s):
        for h in HALVES:
            q_s[s, h, :, NOPE:QK] = qr_s[s, :, part(h, ROPE)]
            qt_s[s, h] = q_s[s, h, :, :QK].T

    def place_k(s):
        for h in HALVES:
            rope = kr_s[s, :, part(h, ROPE)]
            k_s[s, h, :, NOPE:] = jnp.concatenate([rope, rope], axis=1)
            kt_s[s, h, :QK] = k_s[s, h, :, :QK].T

    def place_do(s):
        for h in HALVES:
            dot_s[s, h] = do_s[s, h, :, :VAL].T

    for h in HALVES:
        kt_s[row, h, :QK] = k_s[row, h, :, :QK].T
    place_do(col)
    lax.fori_loop(0, GROUP, clear, 0)

    def diagonal_half(ks, qs):
        return jnp.where((ks < row) | ((ks == row) & (col <= qs)), 0, 1)

    def two_blocks(ks, qs):
        h = diagonal_half(ks, qs)
        return (ks, qs, 0, 1), (ks, qs, h, h)

    own_blocks = [(row, col, kh, qh) for kh in HALVES for qh in HALVES if kh <= qh]

    def f_blocks(t):
        a, b = GROUP - 1, 0
        end = T_LAST
        for t0, a0, na, b0, nb, inner in RECTS[::-1]:
            u = t - t0
            pa, pb = (a0 + u % na, b0 + u // na) if inner else (a0 + u // nb, b0 + u % nb)
            a, b = jnp.where(t < end, pa, a), jnp.where(t < end, pb, b)
            end = t0
        return two_blocks(col_slot(a), jnp.where(t < T_LAST, row_slot(b), t - T_LAST))

    def f_scores(sc, blk):
        ks, qs, kh, qh = blk
        sc[:] = mm(k_s[ks, kh, :, :QK], qt_s[qs, qh])

    def f_use(sc, blk):
        ks, qs, kh, qh = blk
        s = sc[:]
        if isinstance(kh, int) and kh == qh:
            keys = lax.broadcasted_iota(jnp.int32, s.shape, 0)
            s = jnp.where(keys <= lax.broadcasted_iota(jnp.int32, s.shape, 1), s, NEG_BIG)
        m0 = m_s[qs, qh]
        m1 = jnp.maximum(m0, jnp.max(s, axis=0, keepdims=True))
        p = jnp.exp2((s - m1) * EXP2_SCALE)
        alpha = jnp.exp2((m0 - m1) * EXP2_SCALE)
        l_s[qs, qh] = l_s[qs, qh] * alpha + jnp.sum(p, axis=0, keepdims=True)
        m_s[qs, qh] = m1
        ot_s[qs, qh] = ot_s[qs, qh] * alpha + mm(vt_s[ks, kh, :VAL], p.astype(BF))

    def own_f():
        for blk in own_blocks:
            f_scores(sc0, blk)
            f_use(sc0, blk)

    own_f()

    def stats_copies(slot, n):
        return remote([(st_s.at[slot], st_r.at[slot, col])], st_send.at[slot, pl.ds(n - 1, 1)], st_recv.at[pl.ds(slot, 1)], row_dev(n))

    def make_stats(qs):
        for h in HALVES:
            d = jnp.sum(ot_s[qs, h] * dot_s[qs, h].astype(F32), axis=0, keepdims=True)
            for j in range(BLOCKS):
                c = part(j, LANES)
                for i, v in enumerate((m_s[qs, h, :, c], l_s[qs, h, :, c], d[:, c])):
                    st_s[qs, part(GROUP * i + BLOCKS * h + j, 1)] = v

    def start_stats(qs):
        for n in PEERS:
            start(stats_copies(qs, n))
        st_r[qs, col] = st_s[qs]

    def f_arrive(t):
        @pl.when(among(t, tuple(sorted({*Q_STEPS, *K_STEPS, *DO_STEPS, T_RELAY, T_OWN_DO, T_RELAY_DO}))))
        def _():
            @pl.when(among(t, Q_STEPS))
            def _():
                rank = at(t, Q_STEPS, PEERS)

                @pl.when(rank != RING)
                def _():
                    wait_q(rank)
                place_q(row_slot(rank))

            @pl.when(among(t, K_STEPS))
            def _():
                rank = at(t, K_STEPS, PEERS)

                @pl.when(rank != RING)
                def _():
                    wait_k(rank)
                place_k(col_slot(rank))

            @pl.when(among(t, DO_STEPS))
            def _():
                rank = at(t, DO_STEPS, DO_RANKS)
                wait_do(rank)
                place_do(row_slot(rank))

            @pl.when(t == T_RELAY)
            def _():
                wait_q(RING)
                for n in range(FAR):
                    start(pair_copies(*q_kind, n))
                wait_k(RING)
                for n in range(FAR):
                    start(pair_copies(*k_kind, n))

            @pl.when(t == T_OWN_DO)
            def _():
                for n in first_copies:
                    start(own_copies(*do_kind, n))

            @pl.when(t == T_RELAY_DO)
            def _():
                wait_do(RING)
                for n in range(FAR):
                    start(pair_copies(*do_kind, n))
                place_do(row_slot(RING))

    for t in NEIGHBOURS:
        f_arrive(t)
    for sc, blk in zip((sc0, sc1), f_blocks(1)):
        f_scores(sc, blk)

    def f_half(t, used, made):
        b1, b2 = f_blocks(t)
        n1, n2 = f_blocks(jnp.minimum(t + 1, T_END - 1))
        f_scores(made[0], n1)
        f_use(used[0], b1)
        f_scores(made[1], n2)
        f_use(used[1], b2)

        @pl.when(t >= T_LAST)
        def _():
            @pl.when(t > T_LAST)
            def _():
                start_stats(t - T_LAST - 1)

            make_stats(t - T_LAST)

        f_arrive(t + TWO)

    def f_step(u, carry):
        t = TWO * u + 1
        f_half(t, (sc0, sc1), (dp0, dp1))

        @pl.when(t < T_END - 1)
        def _():
            f_half(t + 1, (dp0, dp1), (sc0, sc1))
        return carry

    lax.fori_loop(0, T_END // TWO, f_step, 0)
    start_stats(GROUP - 1)

    def o_refs(slot, buf):
        return [(ot_s.at[slot, h], buf.at[pl.ds(h * VAL, VAL)]) for h in HALVES]

    def o_copies(s):
        d = (s // RING) ^ y0
        return remote(o_refs(s, xo.at[d, x]), xo_send.at[s], xo_recv.at[d, x], {'cp': GROUP * row + RING * y0 + s % RING})

    def o_pair():
        return remote(o_refs(row_slot(RING), po), po_send, po_recv, row_dev(RING))

    def dq_srcs(s, p):
        r = pl.ds(p * ROWS, ROWS)
        return [dq_s.at[s, 0, r], dq_s.at[s, 1, r], dqr_s.at[s, r]]

    def dq_dsts(buf):
        return [buf.at[:, pl.ds(LANES * j, LANES)] for j in range(3)]

    def kv_srcs(s, h):
        return [dk_s.at[s, h], dv_s.at[s, h]]

    def kv_dsts(buf):
        return [buf.at[pl.ds(0, QK)], buf.at[pl.ds(QK, VAL)]]

    dq_near, dq_far, dq_across = ring_sums(row_slot, row_dev, dq_srcs, dq_dsts, (xq, xqv, pq), q_sums_sems)
    kv_near, kv_far, kv_across = ring_sums(col_slot, col_dev, kv_srcs, kv_dsts, (zkv, zkvv, pkv), kv_sums_sems)

    def local(pairs, n=0):
        return [pltpu.make_async_copy(src, dst, loc.at[n + i]) for i, (src, dst) in enumerate(pairs)]

    def o_local(d):
        return local([(xo.at[d, (x + gray(r)) % RING], stg.at[pl.ds(HALF * (r - 1), HALF // TWO)]) for r in range(1, RING)])

    def fetch_o(d):
        for r in range(1, RING):
            s = (x + gray(r)) % RING
            landed(remote(o_refs(0, xo.at[d, s]), xo_send.at[r], xo_recv.at[d, s], row_dev(r)))
        start(o_local(d))

    def add_o(slot, d):
        done(o_local(d))
        for h in HALVES:
            ot_s[slot, h] = ot_s[slot, h] + sum(stg[HALF * n + h * VAL:HALF * n + (h + 1) * VAL] for n in range(FAR))

    def kv_local(d, h):
        return local([(zkv.at[d, n, h], stg.at[pl.ds(KV * n, KV)]) for n in HALVES])

    def fetch_kv(d, h):
        for r in NEIGHBOURS:
            landed(kv_near(RING * d + r, h))
        start(kv_local(d, h))

    def add_kv(slot, d, h):
        done(kv_local(d, h))
        dk_s[slot, h] = dk_s[slot, h] + (stg[:QK] + stg[KV:KV + QK])
        dv_s[slot, h] = dv_s[slot, h] + (stg[QK:KV] + stg[KV + QK:KV + KV])

    def kv_via_local(d):
        return local([(zkvv.at[d, h], stg.at[pl.ds(KV * h, KV)]) for h in HALVES])

    def fetch_kv_via(d):
        for h in HALVES:
            landed(kv_far(d, h))
        start(kv_via_local(d))

    def add_kv_via(d):
        done(kv_via_local(d))
        for h in HALVES:
            slot, u = col_slot(RING * d + 1 + h), KV * h
            dk_s[slot, h] = dk_s[slot, h] + stg[u:u + QK]
            dv_s[slot, h] = dv_s[slot, h] + stg[u + QK:u + KV]

    def dq_stage(n, p):
        return stg.at[pl.ds(HALF * n + ROWS * p, ROWS), pl.ds(0, 3 * LANES)]

    def add_dq(slot, p, ns):
        r = part(p, ROWS)
        for j in range(3):
            c = part(j, LANES)
            total = sum(stg[HALF * n + ROWS * p:HALF * n + ROWS * (p + 1), c] for n in ns)
            if j < TWO:
                dq_s[slot, j, r] = dq_s[slot, j, r] + total
            else:
                dqr_s[slot, r] = dqr_s[slot, r] + total

    def sum_dq_via(d):
        for p in HALVES:
            landed(dq_far(d, p))
        copies = local([(xqv.at[d, p], dq_stage(0, p)) for p in HALVES])
        start(copies)
        done(copies)
        for p in HALVES:
            add_dq(row_slot(RING * d + 1 + p), p, (0,))

    def dq_arrived(d):
        for p in HALVES:
            for r in NEIGHBOURS:
                landed(dq_near(RING * d + r, p))
        return [(xq.at[d, n, p], dq_stage(n, p)) for n in HALVES for p in HALVES]

    def columns(v):
        flat = jnp.concatenate([v[part(j, 1)] for j in range(BLOCKS)], axis=1)
        hi = flat.astype(BF).astype(F32)
        mid = (flat - hi).astype(BF).astype(F32)
        return jnp.concatenate([hi, mid, flat - hi - mid, jnp.zeros((AUG - 3, HALF), F32)], axis=0).T.astype(BF)

    def wait_stats(qs):
        others = st_r.at[qs, pl.ds(0, len(PEERS))]
        pltpu.make_async_copy(others, others, st_recv.at[qs]).wait()

    def prepare(qs):
        wait_stats(qs)
        m, l, d = (st_r[qs, :, part(i, GROUP)] for i in range(3))
        m_all = jnp.max(m, axis=0)
        w = jnp.exp2((m - m_all[None]) * EXP2_SCALE)
        l_all = jnp.sum(w * l, axis=0)
        inv = 1.0 / l_all
        delta = jnp.sum(w * d, axis=0) * inv
        lse = m_all + jnp.log2(l_all) * (1.0 / EXP2_SCALE)
        mine = jnp.exp2((st_s[qs, :GROUP] - m_all) * EXP2_SCALE) * inv
        for h in HALVES:
            q_s[qs, h, :, QK:] = columns(-lse[part(h, BLOCKS)])
            do_s[qs, h, :, VAL:] = columns(-delta[part(h, BLOCKS)])
            for j in range(BLOCKS):
                c = part(j, LANES)
                ot_s[qs, h, :, c] = ot_s[qs, h, :, c] * mine[part(BLOCKS * h + j, 1)]

    def b_blocks(t):
        ks = col_slot(jnp.where(t < T_OWN, order(t // GROUP, K_ORDER), 0))
        qs = jnp.where(t < T_OWN, t % GROUP, row_slot(order(t - T_OWN, Q_ORDER)))
        b1, b2 = two_blocks(ks, qs)
        split = (t >= T_SPLIT) & (t < T_OWN)
        u = t - T_SPLIT
        late = u >= RING
        s = TWO * (u % RING)
        h = diagonal_half(ks, 0)
        kh, qh = jnp.where(late, h, 0), jnp.where(late, h, 1)
        pick = lambda a, b: tuple(jnp.where(split, i, j) for i, j in zip(a, b))
        return pick((ks, s, kh, qh), b1), pick((ks, s + 1, kh, qh), b2)

    def b_scores(sc, dp, blk):
        ks, qs, kh, qh = blk
        sc[:] = mm(q_s[qs, qh], kt_s[ks, kh])
        dp[:] = mm(do_s[qs, qh], vt_s[ks, kh])

    def b_elem(sc, dp, pr, ds, mask=False):
        p = jnp.exp2(sc[:] * EXP2_SCALE)
        if mask:
            rows = lax.broadcasted_iota(jnp.int32, p.shape, 0)
            p = jnp.where(lax.broadcasted_iota(jnp.int32, p.shape, 1) <= rows, p, 0.0)
        pr[:] = p.astype(BF)
        ds[:] = (p * dp[:]).astype(BF)

    def b_grads(pr, ds, blk):
        ks, qs, kh, qh = blk
        p = pr[:]
        g = ds[:]
        dv_s[ks, kh] += mm(dot_s[qs, qh], p)
        dk_s[ks, kh] += mm(qt_s[qs, qh], g)
        dq = mm(g, k_s[ks, kh])
        dq_s[qs, qh] += dq[:, :NOPE]
        side = lax.broadcasted_iota(jnp.int32, (1, LANES), 1) // ROPE
        dqr_s[qs] += jnp.where(side == qh, dq[:, NOPE:], 0.0)

    early_half = 1 - diagonal_half(col_slot(K_ORDER[-1]), 0)

    def b_events(t):
        @pl.when((t <= GROUP) | among(t, (*T_VIA, *T_FETCH, *T_ADD, *T_NEAR, T_NEAR_MID, T_NEAR_LAST, T_PAIR_O - 1, T_PAIR_O, T_PAIR_O + 1, T_VIA_Q, T_Q_FIVE, T_Q_SIX)) | among(t, tuple(v + i for v in T_PAIR_KV for i in range(3))))
        def _():
            @pl.when((t < GROUP - 1) & (t % TWO == 1))
            def _():
                for n in NEIGHBOURS:
                    prepare(t + n)

            @pl.when((t <= GROUP) & ((t - 1) % RING != x))
            def _():
                start(o_copies(t - 1))

            @pl.when(among(t, T_VIA))
            def _():
                for h in HALVES:
                    start(kv_far(at(t, T_VIA, (1, 0)), h))

            @pl.when(among(t, T_FETCH))
            def _():
                fetch_kv_via(at(t, T_FETCH, (1, 0)))

            @pl.when(among(t, T_ADD))
            def _():
                add_kv_via(at(t, T_ADD, (1, 0)))

            @pl.when(among(t, T_NEAR))
            def _():
                for h in HALVES:
                    start(kv_near(at(t, T_NEAR, NEAR), h))

            @pl.when(t == T_NEAR_MID)
            def _():
                start(kv_near(K_ORDER[-1], early_half))

            @pl.when(t == T_NEAR_LAST)
            def _():
                start(kv_near(K_ORDER[-1], 1 - early_half))

            @pl.when(t == T_VIA_Q)
            def _():
                for p in HALVES:
                    start(dq_far(1, p))

            @pl.when(t == T_Q_FIVE)
            def _():
                start(dq_near(5, 1))

            @pl.when(t == T_Q_SIX)
            def _():
                start(dq_near(6, 0))

            @pl.when(t == T_PAIR_O - 1)
            def _():
                fetch_o(1)

            @pl.when(t == T_PAIR_O)
            def _():
                add_o(row_slot(RING), 1)

            @pl.when(t == T_PAIR_O + 1)
            def _():
                start(o_pair())

            for h, v in enumerate(T_PAIR_KV):
                @pl.when(t == v)
                def _():
                    fetch_kv(1, h)

                @pl.when(t == v + 1)
                def _():
                    add_kv(col_slot(RING), 1, h)

                @pl.when(t == v + TWO)
                def _():
                    start(kv_across(h))

    def b_step(t, carry):
        b1, b2 = b_blocks(t)
        b_scores(sc1, dp1, b2)
        b_elem(sc0, dp0, pr0, ds0)
        b_grads(pr1, ds1, b_blocks(jnp.maximum(t - 1, 0))[1])
        b_scores(sc0, dp0, b_blocks(jnp.minimum(t + 1, T_END - TWO))[0])
        b_elem(sc1, dp1, pr1, ds1)
        b_grads(pr0, ds0, b1)
        b_events(t + 1)
        return carry

    for ref in (pr1, ds1):
        ref[:] = jnp.zeros(ref.shape, BF)
    for s in HALVES:
        prepare(s)
    b_scores(sc0, dp0, b_blocks(0)[0])
    lax.fori_loop(0, T_END - 1, b_step, 0)
    b_grads(pr1, ds1, b_blocks(T_END - TWO)[1])

    def own_b():
        for blk in own_blocks:
            b_scores(sc0, dp0, blk)
            b_elem(sc0, dp0, pr0, ds0, mask=blk[TWO] == blk[3])
            b_grads(pr0, ds0, blk)

    fetch_o(0)
    own_b()

    def finish_o():
        add_o(col, 0)
        landed(o_pair())
        last_o = local([(po, sc0.at[pl.ds(0, HALF // TWO)])])
        start(last_o)
        for n in range(RING):
            left(own_copies(*do_kind, n))
        done(last_o)
        for h in HALVES:
            do_s[col, h, :, :VAL] = (ot_s[col, h] + sc0[part(h, VAL)]).T.astype(BF)

    finish_o()
    sum_dq_via(1)
    for pr, h in zip((pr0, pr1), HALVES):
        pr[:] = c_in[h].T
    start(dq_near(5, 0) + dq_near(6, 1))
    finals = [pltpu.make_async_copy(do_s.at[col, :, :, :VAL], out_o, outs.at[0])]
    start(finals)

    def finish_dkv():
        sums = None
        for h in HALVES:
            fetch_kv(0, h)
            landed(kv_across(h))
            pair = local([(pkv.at[h], sc0.at[pl.ds(0, KV)])], TWO)
            start(pair)
            add_kv(row, 0, h)
            done(pair)
            dk = (dk_s[row, h] + sc0[:QK]) * SCALE
            dv = dv_s[row, h] + sc0[QK:KV]
            rope_s[:, part(h, HALF)] = dk[NOPE:]
            kv = jnp.concatenate([dk[:NOPE].T, dv.T], axis=1)
            (dp0, dp1)[h][:, :NOPE + VAL] = kv
            product = mm((pr0, pr1)[h][:].astype(F32), kv)
            sums = product if sums is None else sums + product
        w_s[0] = sums[:, :NOPE]
        w_s[1] = sums[:, NOPE:]

    finish_dkv()

    def w_swap(src, dst, n):
        return remote([(src, dst)], w_send.at[pl.ds(n, 1)], w_recv.at[pl.ds(n, 1)], mate)

    def strip(d):
        return rows_of(d, STRIP)

    def to_all(n, src, dst):
        to_others(lambda d: pltpu.make_async_remote_copy(src(d), dst, strip_send.at[n], strip_recv.at[n], device_id={'cp': d}).start())

    def all_of(sem, n):
        strips = wr_r.at[pl.ds(0, CHIPS - 1)]
        pltpu.make_async_copy(strips, strips, sem.at[n]).wait()

    first = w_swap(w_s.at[1 - core], ws_r, 0)
    start(first + dq_far(0, 0) + dq_far(0, 1))

    def finish_dq_pair():
        copies = local(dq_arrived(1))
        start(copies)
        done(copies)
        for p in HALVES:
            add_dq(row_slot(RING), p, HALVES)

    finish_dq_pair()

    def finish_c():
        w_all = jnp.concatenate([wk_in[:], wv_in[:]], axis=1).astype(F32)
        for kv, out in ((dp0, sc0), (dp1, sc1)):
            out[:] = mm_t(kv[:, :NOPE + VAL], w_all)

    finish_c()
    outputs = [(sc0, out_c.at[0]), (sc1, out_c.at[1]), (rope_s, out_r)]
    more = [pltpu.make_async_copy(src, dst, outs.at[1 + n]) for n, (src, dst) in enumerate(outputs)]
    start(more)
    finals += more


    def w_one():
        landed(first)
        wr_s[:] = w_s[core] + ws_r[:]

    w_one()
    to_all(0, lambda d: wr_s.at[strip(d)], wr_r.at[me])
    start(dq_across(0) + dq_near(1, 1) + dq_near(2, 0))
    wr_r[me] = wr_s[strip(me)]
    sum_dq_via(0)
    left(first)

    def w_two():
        all_of(strip_recv, 0)
        w_s[core, strip(me)] = jnp.sum(wr_r[:], axis=0)

    w_two()
    mine = w_s.at[core, strip(me)]
    to_all(1, lambda d: mine, mine)
    start(dq_across(1) + dq_near(1, 0) + dq_near(2, 1))

    def w_three():
        all_of(strip_recv, 1)

    w_three()
    last = w_swap(w_s.at[core], wl_r, 1)
    start(last)

    def finish_dq():
        pairs = dq_arrived(0)
        for p in HALVES:
            landed(dq_across(p))
        copies = local(pairs + [(pq.at[p], dq_stage(TWO, p)) for p in HALVES])
        start(copies)
        done(copies)
        for p in HALVES:
            add_dq(col, p, range(3))
        for h in HALVES:
            q_out_s[:NOPE, part(h, HALF)] = (dq_s[col, h] * SCALE).T
        rope = (dqr_s[col] * SCALE).T
        for h in HALVES:
            q_out_s[NOPE:, part(h, HALF)] = rope[part(h, ROPE)]

    def w_five():
        landed(last)
        w_s[1 - core] = wl_r[:]

    w_five()
    more = [pltpu.make_async_copy(src, dst, outs.at[RING + n]) for n, (src, dst) in enumerate([(w_s.at[0], out_uk), (w_s.at[1], out_uv)])]
    start(more)
    finals += more
    finish_dq()
    q_out = pltpu.make_async_copy(q_out_s, out_q, outs.at[RING + TWO])
    q_out.start()

    left(last)
    for n in HALVES:
        all_of(strip_send, n)
    for r in PEERS:
        for s in range(GROUP):
            left(stats_copies(s, r))
        if r != RING:
            left(o_copies(row_slot(r)))
        if r % RING in NEIGHBOURS:
            for p in HALVES:
                left(dq_near(r, p) + kv_near(r, p))
    for p in HALVES:
        left(dq_across(p) + kv_across(p))
        for d in HALVES:
            left(dq_far(d, p) + kv_far(d, p))
    left(o_pair())
    for n in range(RING):
        left(own_copies(*q_kind, n) + own_copies(*k_kind, n))
    for n in range(FAR):
        left(pair_copies(*q_kind, n) + pair_copies(*k_kind, n) + pair_copies(*do_kind, n))
    done(finals + [q_out])


def core_call(c, kpe, q, wk, wv, do):
    dma = lambda *s: pltpu.SemaphoreType.DMA(s)
    shape = jax.ShapeDtypeStruct
    per = (GROUP, TWO)
    wide = lambda *s: pltpu.VMEM(per + s, BF)
    sums = lambda *s: pltpu.VMEM(per + s, F32)
    f32 = lambda *s: pltpu.VMEM(s, F32)
    packed = pltpu.VMEM((GROUP, HALF, LANES), BF)

    def sum_sems(n):
        return (dma(GROUP, TWO, n), dma(TWO, TWO, TWO, n), dma(TWO, TWO, n), dma(TWO, TWO, n), dma(TWO, n), dma(TWO, n))

    def sum_bufs(*s):
        return [shape((TWO, TWO, TWO, *s), F32), shape((TWO, TWO, *s), F32), shape((TWO, *s), F32)]

    square = (HALF, HALF)
    scratch = [
        wide(HALF, QK + AUG), packed, wide(HALF, QK + ROPE), packed, wide(VAL + AUG, HALF), wide(HALF, VAL + AUG),
        wide(QK, HALF), wide(QK + AUG, HALF), wide(VAL, HALF),
        sums(VAL, HALF), sums(1, HALF), sums(1, HALF),
        sums(HALF, NOPE), f32(GROUP, HALF, LANES), sums(QK, HALF), sums(VAL, HALF),
        f32(GROUP, 3 * GROUP, LANES), f32(GROUP, GROUP, 3 * GROUP, LANES), f32(3 * HALF, HALF),
        f32(TWO, LATENT, NOPE), f32(LATENT, NOPE), f32(LATENT, NOPE), f32(ROPE, TWO * HALF), f32(QK, TWO * HALF),
        f32(LATENT, NOPE), f32(CHIPS, STRIP, NOPE),
        *[f32(*square)] * RING, *[pltpu.VMEM(square, BF)] * RING,
        dma(len(PEERS), TWO), dma(GROUP, TWO), dma(len(PEERS), 3), dma(GROUP, 3), dma(len(PEERS), 1), dma(GROUP, 1),
        dma(GROUP, len(PEERS)), dma(GROUP), dma(GROUP, TWO), dma(TWO, RING, TWO), dma(TWO), dma(TWO),
        sum_sems(3), sum_sems(TWO), dma(GROUP), dma(GROUP), dma(TWO), dma(TWO), dma(TWO), dma(TWO),
    ]
    results = [
        shape((TWO, HALF, VAL), BF), shape((QK, TWO * HALF), F32), shape((TWO, HALF, LATENT), F32), shape((ROPE, TWO * HALF), F32),
        shape((LATENT, NOPE), F32), shape((LATENT, VAL), F32),
    ]
    landing = [shape((TWO, RING, TWO * VAL, HALF), F32), shape((TWO * VAL, HALF), F32), *sum_bufs(ROWS, 3 * LANES), *sum_bufs(KV, HALF)]
    anywhere = pl.BlockSpec(memory_space=pl.ANY)
    return pl.pallas_call(
        core_kernel,
        out_shape=results + landing,
        in_specs=[pl.BlockSpec(memory_space=pltpu.VMEM)] * 6,
        out_specs=[anywhere] * len(results + landing),
        scratch_shapes=scratch,
        compiler_params=pltpu.CompilerParams(collective_id=0, has_side_effects=True, vmem_limit_bytes=67043328),
        name='core',
    )(c, kpe, q, wk, wv, do)[:len(results)]


def solution(mesh):
    batch = ('pod', 'data')
    token_spec = P(batch, 'cp')
    sum_spec = P('pod')

    def per_device(c_latent, k_rope, queries, w_uk, w_uv, d_out):
        halves = lambda a: a.reshape(TWO, HALF, a.shape[-1])
        o, gq, gc, gr, guk, guv = core_call(halves(c_latent), k_rope[0].T, queries[0, :, 0].T, w_uk[:, 0], w_uv[:, 0], halves(d_out))
        return o.reshape(d_out.shape), gq.T.reshape(queries.shape), gc.reshape(c_latent.shape), gr.T.reshape(k_rope.shape), guk[:, None], guv[:, None]

    return jax.shard_map(per_device, mesh=mesh, in_specs=(token_spec, token_spec, token_spec, P(), P(), token_spec), out_specs=(token_spec, token_spec, token_spec, token_spec, sum_spec, sum_spec), check_vma=False)
```

time: 2770 us -> 258 us (0.09)
  the two profiles are of different devices: /device:TPU:0 before, /device:TPU:1 now
where the time goes in v3:
time: 258 us
  Pallas kernels  250 us (97%)
  local copies, waits for them, and re-layouts  7.39 us (3%)
    pallas_call x1, Pallas kernels, core_call(): pl.pallas_call(core_kernel, out_shape=results + landing, in_specs=[pl.Blo...  250 us
    unnamed x14, local copies, waits for them, and re-layouts  7.39 us

profile of v3, /device:TPU:1, one launch (start us, length us, event | category | flops | bytes accessed | tf_op | source)
XLA Modules:
  0.0 257.9 jit_solution(9948841868222941119)
XLA Ops:
  0.6 249.8 %core.1 = (bf16[2,512,128]{2,1,0:T(8,128)(2,1)}, f32[192,1024]{1,0:T(8,128)}, f32[2,512,512]{2,1,0:T(8,128)}, f32[64,1024]{1,0:T(8,128)}, f32[512,128]{1,0:T(8,1...) custom-call(bf16[2,512,512]{2,1,0:T(8,128)(2,1)} %bitcast.25, ...), custom_call_target="tpu_custom_call" | custom-call | tf_op jit(solution)/shard_map/core/pallas_call | solution.py:859
  250.5 0.0 copy-start
  250.5 1.8 copy.20
  252.3 0.0 copy-start.3
  252.3 2.1 copy.21
  254.4 0.0 copy-done
  254.4 0.0 copy-start.2
  254.4 0.0 copy-start.1
  254.4 1.3 copy.22
  255.7 0.0 copy-done.3
  255.8 0.7 copy.23
  256.5 0.0 copy-done.2
  256.5 0.7 copy.24
  257.2 0.0 copy-done.1
  257.2 0.7 copy.25
Async XLA Ops:
  250.5 4.0 %copy-start = (f32[2,512,512]{2,1,0:T(8,128)S(1)}, f32[2,512,512]{2,1,0:T(8,128)}, u32[]{:S(2)}) copy-start(f32[2,512,512]{2,1,0:T(8,128)} %get-tuple-element.14) | copy-start | bytes 6291460
  252.3 3.5 %copy-start.3 = (f32[64,1024]{1,0:T(8,128)S(1)}, f32[64,1024]{1,0:T(8,128)}, u32[]{:S(2)}) copy-start(f32[64,1024]{1,0:T(8,128)} %get-tuple-element.15) | copy-start | bytes 786436
  254.4 2.0 copy-start.2
  254.4 2.7 %copy-start.1 = (f32[512,128]{1,0:T(8,128)S(1)}, f32[512,128]{1,0:T(8,128)}, u32[]{:S(2)}) copy-start(f32[512,128]{1,0:T(8,128)} %get-tuple-element.17) | copy-start | bytes 786436

commit v4 on v3

--- a/solution.py
+++ b/solution.py
@@ -37,16 +37,18 @@
 T_LAST = 56
 T_END = 64
 RECTS = ((1, 0, 1, 1, 2, False), (3, 1, 2, 0, 3, False), (9, 0, 3, 3, 2, True), (15, 3, 2, 0, 5, False), (25, 0, 5, 5, 3, True), (40, 5, 2, 0, 8, False))
-K_ORDER = (7, 3, 5, 6, 4, 1, 2)
-Q_ORDER = (7, 5, 6, 3, 1, 2, 4)
-T_SPLIT, T_OWN = 48, 56
-T_VIA = (9, 17)
-T_FETCH, T_ADD = (21, 31), (22, 32)
-T_NEAR, NEAR = (25, 33, 49), (5, 6, 1)
-T_NEAR_MID, T_NEAR_LAST = 53, 57
-T_PAIR_O = 38
-T_PAIR_KV = (46, 54)
-T_VIA_Q, T_Q_FIVE, T_Q_SIX = 58, 59, 60
+K_ORDER = (7, 5, 6, 4, 3, 1, 2)
+Q_FIRST, Q_REST = (7, 5, 6), (3, 1, 2, 4, 0)
+T_SPLIT, T_MIX = 48, 52
+M_REST, M_OWN = 9, 14
+T_VIA = (9, 41)
+T_FETCH, T_ADD = (21, 53), (22, 54)
+T_NEAR, NEAR = (23, 25), (5, 6)
+T_ONE = (49, 55)
+T_NEAR_MID, T_NEAR_LAST = 55, 60
+T_PAIR_O = 56
+T_PAIR_KV = (36, 45)
+T_VIA_Q, T_Q_FIVE, T_Q_SIX = 54, 56, 57
 
 
 def mm(a, b):
@@ -100,6 +102,21 @@
         c.wait()
 
 
+class Remote:
+    def __init__(self, pairs, send, recv, dev, ref):
+        self.pairs, self.send, self.recv, self.dev, self.ref = pairs, send, recv, dev, ref
+
+    def start(self):
+        for src, dst in self.pairs:
+            pltpu.make_async_remote_copy(src, dst, self.send, self.recv, device_id=self.dev).start()
+
+    def wait_recv(self):
+        pltpu.make_async_copy(self.ref, self.ref, self.recv).wait()
+
+    def wait_send(self):
+        pltpu.make_async_copy(self.ref, self.ref, self.send).wait()
+
+
 def landed(copies):
     for c in copies:
         c.wait_recv()
@@ -110,23 +127,23 @@
         c.wait_send()
 
 
-def remote(pairs, send, recv, dev):
-    return [pltpu.make_async_remote_copy(src, dst, send.at[n], recv.at[n], device_id=dev) for n, (src, dst) in enumerate(pairs)]
-
-
-def ring_sums(slot, dev, srcs, dsts, bufs, sems):
+def remote(pairs, send, recv, dev, ref):
+    return [Remote(pairs, send, recv, dev, ref)]
+
+
+def ring_sums(slot, dev, far_rank, srcs, dsts, bufs, sems, ref):
     main, via, pair = bufs
     main_send, main_recv, via_send, via_recv, pair_send, pair_recv = sems
 
     def near(rank, p):
         d, n = rank // RING, rank % RING - 1
-        return remote(zip(srcs(slot(rank), p), dsts(main.at[d, n, p])), main_send.at[rank, p], main_recv.at[d, n, p], dev(n + 1))
+        return remote(zip(srcs(slot(rank), p), dsts(main.at[d, n, p])), main_send.at[rank, p], main_recv.at[d, n, p], dev(n + 1), ref)
 
     def far(d, p):
-        return remote(zip(srcs(slot(RING * d + FAR), p), dsts(via.at[d, p])), via_send.at[d, p], via_recv.at[d, p], dev(p + 1))
+        return remote(zip(srcs(slot(RING * d + FAR), p), dsts(via.at[d, p])), via_send.at[d, p], via_recv.at[d, p], dev(far_rank(d, p)), ref)
 
     def across(p):
-        return remote(zip(srcs(slot(RING), p), dsts(pair.at[p])), pair_send.at[p], pair_recv.at[p], dev(RING))
+        return remote(zip(srcs(slot(RING), p), dsts(pair.at[p])), pair_send.at[p], pair_recv.at[p], dev(RING), ref)
 
     return near, far, across
 
@@ -185,19 +202,22 @@
 
     pl.semaphore_wait(barrier, CHIPS)
 
+    def like(n):
+        return qr_s.at[pl.ds(0, n)]
+
     def q_copies(n, slot, dev):
         refs = [q_s.at[slot, :, :, :NOPE], qr_s.at[slot]]
-        return remote(zip(refs, refs), q_send.at[n], q_recv.at[slot], dev)
+        return remote(zip(refs, refs), q_send.at[n], q_recv.at[slot], dev, like(3))
 
     def k_copies(n, slot, dev):
         refs = [k_s.at[slot, :, :, :NOPE], kr_s.at[slot], vt_s.at[slot, :, :VAL]]
-        return remote(zip(refs, refs), k_send.at[n], k_recv.at[slot], dev)
+        return remote(zip(refs, refs), k_send.at[n], k_recv.at[slot], dev, like(5))
 
     def do_copies(n, slot, dev):
         ref = do_s.at[slot, :, :, :VAL]
-        return remote([(ref, ref)], do_send.at[n], do_recv.at[slot], dev)
-
-    first_copies = (FAR, *range(FAR))
+        return remote([(ref, ref)], do_send.at[n], do_recv.at[slot], dev, like(TWO))
+
+    first_copies = (FAR, 0, 1)
 
     def own_copies(copies, slot, dev, n):
         return copies(n, slot(0), dev(n + 1))
@@ -300,7 +320,7 @@
     own_f()
 
     def stats_copies(slot, n):
-        return remote([(st_s.at[slot], st_r.at[slot, col])], st_send.at[slot, pl.ds(n - 1, 1)], st_recv.at[pl.ds(slot, 1)], row_dev(n))
+        return remote([(st_s.at[slot], st_r.at[slot, col])], st_send.at[slot], st_recv.at[slot], row_dev(n), st_r.at[slot, pl.ds(0, len(PEERS))])
 
     def make_stats(qs):
         for h in HALVES:
@@ -325,6 +345,10 @@
                 @pl.when(rank != RING)
                 def _():
                     wait_q(rank)
+
+                @pl.when(rank == 1)
+                def _():
+                    start(own_copies(*q_kind, TWO))
                 place_q(row_slot(rank))
 
             @pl.when(among(t, K_STEPS))
@@ -334,6 +358,10 @@
                 @pl.when(rank != RING)
                 def _():
                     wait_k(rank)
+
+                @pl.when(rank == 1)
+                def _():
+                    start(own_copies(*k_kind, TWO))
                 place_k(col_slot(rank))
 
             @pl.when(among(t, DO_STEPS))
@@ -353,7 +381,7 @@
 
             @pl.when(t == T_OWN_DO)
             def _():
-                for n in first_copies:
+                for n in (*first_copies, TWO):
                     start(own_copies(*do_kind, n))
 
             @pl.when(t == T_RELAY_DO)
@@ -365,12 +393,12 @@
 
     for t in NEIGHBOURS:
         f_arrive(t)
-    for sc, blk in zip((sc0, sc1), f_blocks(1)):
+    blocks = f_blocks(jnp.int32(1))
+    for sc, blk in zip((sc0, sc1), blocks):
         f_scores(sc, blk)
 
-    def f_half(t, used, made):
-        b1, b2 = f_blocks(t)
-        n1, n2 = f_blocks(jnp.minimum(t + 1, T_END - 1))
+    def f_half(t, used, made, b1, b2):
+        n1, n2 = after = f_blocks(jnp.minimum(t + 1, T_END - 1))
         f_scores(made[0], n1)
         f_use(used[0], b1)
         f_scores(made[1], n2)
@@ -385,28 +413,31 @@
             make_stats(t - T_LAST)
 
         f_arrive(t + TWO)
+        return after
 
     def f_step(u, carry):
         t = TWO * u + 1
-        f_half(t, (sc0, sc1), (dp0, dp1))
+        after = f_half(t, (sc0, sc1), (dp0, dp1), *carry)
 
         @pl.when(t < T_END - 1)
         def _():
-            f_half(t + 1, (dp0, dp1), (sc0, sc1))
-        return carry
-
-    lax.fori_loop(0, T_END // TWO, f_step, 0)
+            f_half(t + 1, (dp0, dp1), (sc0, sc1), *after)
+        return f_blocks(jnp.minimum(t + TWO, T_END - 1))
+
+    lax.fori_loop(0, T_END // TWO, f_step, blocks)
     start_stats(GROUP - 1)
+
+    o_all = stg.at[pl.ds(0, TWO * VAL)]
 
     def o_refs(slot, buf):
         return [(ot_s.at[slot, h], buf.at[pl.ds(h * VAL, VAL)]) for h in HALVES]
 
     def o_copies(s):
         d = (s // RING) ^ y0
-        return remote(o_refs(s, xo.at[d, x]), xo_send.at[s], xo_recv.at[d, x], {'cp': GROUP * row + RING * y0 + s % RING})
+        return remote(o_refs(s, xo.at[d, x]), xo_send.at[s], xo_recv.at[d, x], {'cp': GROUP * row + RING * y0 + s % RING}, o_all)
 
     def o_pair():
-        return remote(o_refs(row_slot(RING), po), po_send, po_recv, row_dev(RING))
+        return remote(o_refs(row_slot(RING), po), po_send.at[0], po_recv.at[0], row_dev(RING), o_all)
 
     def dq_srcs(s, p):
         r = pl.ds(p * ROWS, ROWS)
@@ -421,8 +452,8 @@
     def kv_dsts(buf):
         return [buf.at[pl.ds(0, QK)], buf.at[pl.ds(QK, VAL)]]
 
-    dq_near, dq_far, dq_across = ring_sums(row_slot, row_dev, dq_srcs, dq_dsts, (xq, xqv, pq), q_sums_sems)
-    kv_near, kv_far, kv_across = ring_sums(col_slot, col_dev, kv_srcs, kv_dsts, (zkv, zkvv, pkv), kv_sums_sems)
+    dq_near, dq_far, dq_across = ring_sums(row_slot, row_dev, lambda d, p: RING if d else p + 1, dq_srcs, dq_dsts, (xq, xqv, pq), q_sums_sems, stg.at[pl.ds(0, ROWS * 3 * LANES // HALF)])
+    kv_near, kv_far, kv_across = ring_sums(col_slot, col_dev, lambda d, p: p + 1, kv_srcs, kv_dsts, (zkv, zkvv, pkv), kv_sums_sems, stg.at[pl.ds(0, KV)])
 
     def local(pairs, n=0):
         return [pltpu.make_async_copy(src, dst, loc.at[n + i]) for i, (src, dst) in enumerate(pairs)]
@@ -433,7 +464,7 @@
     def fetch_o(d):
         for r in range(1, RING):
             s = (x + gray(r)) % RING
-            landed(remote(o_refs(0, xo.at[d, s]), xo_send.at[r], xo_recv.at[d, s], row_dev(r)))
+            landed(remote(o_refs(0, xo.at[d, s]), xo_send.at[r], xo_recv.at[d, s], row_dev(r), o_all))
         start(o_local(d))
 
     def add_o(slot, d):
@@ -489,7 +520,7 @@
         start(copies)
         done(copies)
         for p in HALVES:
-            add_dq(row_slot(RING * d + 1 + p), p, (0,))
+            add_dq(row_slot(FAR if d else 1 + p), p, (0,))
 
     def dq_arrived(d):
         for p in HALVES:
@@ -504,8 +535,7 @@
         return jnp.concatenate([hi, mid, flat - hi - mid, jnp.zeros((AUG - 3, HALF), F32)], axis=0).T.astype(BF)
 
     def wait_stats(qs):
-        others = st_r.at[qs, pl.ds(0, len(PEERS))]
-        pltpu.make_async_copy(others, others, st_recv.at[qs]).wait()
+        landed(stats_copies(qs, 1))
 
     def prepare(qs):
         wait_stats(qs)
@@ -524,18 +554,22 @@
                 c = part(j, LANES)
                 ot_s[qs, h, :, c] = ot_s[qs, h, :, c] * mine[part(BLOCKS * h + j, 1)]
 
+    def b_mixed(m):
+        first, rest = m < M_REST, m < M_OWN
+        rank = jnp.where(first, order(m // 3, Q_FIRST), order(jnp.where(rest, m - M_REST, (m - M_OWN) // TWO), Q_REST))
+        ring = jnp.where(first, m % 3, jnp.where(rest, 0, 1)) == 0
+        same = ring | (jnp.where(first, m % 3, 1 + m % TWO) == TWO)
+        ks, qs = jnp.where(ring, col_slot(K_ORDER[-1]), row), row_slot(rank)
+        h = diagonal_half(ks, qs)
+        return ks, qs, jnp.where(same, h, 0), jnp.where(same, h, 1)
+
     def b_blocks(t):
-        ks = col_slot(jnp.where(t < T_OWN, order(t // GROUP, K_ORDER), 0))
-        qs = jnp.where(t < T_OWN, t % GROUP, row_slot(order(t - T_OWN, Q_ORDER)))
-        b1, b2 = two_blocks(ks, qs)
-        split = (t >= T_SPLIT) & (t < T_OWN)
-        u = t - T_SPLIT
-        late = u >= RING
-        s = TWO * (u % RING)
-        h = diagonal_half(ks, 0)
-        kh, qh = jnp.where(late, h, 0), jnp.where(late, h, 1)
-        pick = lambda a, b: tuple(jnp.where(split, i, j) for i, j in zip(a, b))
-        return pick((ks, s, kh, qh), b1), pick((ks, s + 1, kh, qh), b2)
+        b1, b2 = two_blocks(col_slot(order(t // GROUP, K_ORDER)), t % GROUP)
+        pick = lambda c, a, b: tuple(jnp.where(c, i, j) for i, j in zip(a, b))
+        last = col_slot(K_ORDER[-1])
+        u = TWO * (t - T_SPLIT)
+        m = TWO * (t - T_MIX)
+        return tuple(pick(t < T_SPLIT, b, pick(t < T_MIX, (last, u + n, 0, 1), b_mixed(m + n))) for n, b in enumerate((b1, b2)))
 
     def b_scores(sc, dp, blk):
         ks, qs, kh, qh = blk
@@ -564,7 +598,7 @@
     early_half = 1 - diagonal_half(col_slot(K_ORDER[-1]), 0)
 
     def b_events(t):
-        @pl.when((t <= GROUP) | among(t, (*T_VIA, *T_FETCH, *T_ADD, *T_NEAR, T_NEAR_MID, T_NEAR_LAST, T_PAIR_O - 1, T_PAIR_O, T_PAIR_O + 1, T_VIA_Q, T_Q_FIVE, T_Q_SIX)) | among(t, tuple(v + i for v in T_PAIR_KV for i in range(3))))
+        @pl.when((t <= GROUP) | among(t, (*T_VIA, *T_FETCH, *T_ADD, *T_NEAR, *T_ONE, T_NEAR_MID, T_NEAR_LAST, T_PAIR_O - 1, T_PAIR_O, T_PAIR_O + 1, T_VIA_Q, T_Q_FIVE, T_Q_SIX)) | among(t, tuple(v + i for v in T_PAIR_KV for i in range(3))))
         def _():
             @pl.when((t < GROUP - 1) & (t % TWO == 1))
             def _():
@@ -593,6 +627,10 @@
                 for h in HALVES:
                     start(kv_near(at(t, T_NEAR, NEAR), h))
 
+            @pl.when(among(t, T_ONE))
+            def _():
+                start(kv_near(1, at(t, T_ONE, (1, 0))))
+
             @pl.when(t == T_NEAR_MID)
             def _():
                 start(kv_near(K_ORDER[-1], early_half))
@@ -608,11 +646,11 @@
 
             @pl.when(t == T_Q_FIVE)
             def _():
-                start(dq_near(5, 1))
+                start(dq_near(5, 0) + dq_near(5, 1))
 
             @pl.when(t == T_Q_SIX)
             def _():
-                start(dq_near(6, 0))
+                start(dq_near(6, 0) + dq_near(6, 1))
 
             @pl.when(t == T_PAIR_O - 1)
             def _():
@@ -640,23 +678,25 @@
                     start(kv_across(h))
 
     def b_step(t, carry):
-        b1, b2 = b_blocks(t)
+        before, (b1, b2) = carry
+        after = b_blocks(jnp.minimum(t + 1, T_END - TWO))
         b_scores(sc1, dp1, b2)
         b_elem(sc0, dp0, pr0, ds0)
-        b_grads(pr1, ds1, b_blocks(jnp.maximum(t - 1, 0))[1])
-        b_scores(sc0, dp0, b_blocks(jnp.minimum(t + 1, T_END - TWO))[0])
+        b_grads(pr1, ds1, before)
+        b_scores(sc0, dp0, after[0])
         b_elem(sc1, dp1, pr1, ds1)
         b_grads(pr0, ds0, b1)
         b_events(t + 1)
-        return carry
+        return b2, after
 
     for ref in (pr1, ds1):
         ref[:] = jnp.zeros(ref.shape, BF)
     for s in HALVES:
         prepare(s)
-    b_scores(sc0, dp0, b_blocks(0)[0])
-    lax.fori_loop(0, T_END - 1, b_step, 0)
-    b_grads(pr1, ds1, b_blocks(T_END - TWO)[1])
+    blocks = b_blocks(jnp.int32(0))
+    b_scores(sc0, dp0, blocks[0])
+    before, _ = lax.fori_loop(0, T_END - 1, b_step, (blocks[1], blocks))
+    b_grads(pr1, ds1, before)
 
     def own_b():
         for blk in own_blocks:
@@ -664,27 +704,34 @@
             b_elem(sc0, dp0, pr0, ds0, mask=blk[TWO] == blk[3])
             b_grads(pr0, ds0, blk)
 
-    fetch_o(0)
     own_b()
 
     def finish_o():
+        fetch_o(0)
         add_o(col, 0)
         landed(o_pair())
-        last_o = local([(po, sc0.at[pl.ds(0, HALF // TWO)])])
+        last_o = local([(po, stg.at[pl.ds(HALF // TWO, HALF // TWO)])])
         start(last_o)
         for n in range(RING):
             left(own_copies(*do_kind, n))
         done(last_o)
         for h in HALVES:
-            do_s[col, h, :, :VAL] = (ot_s[col, h] + sc0[part(h, VAL)]).T.astype(BF)
-
-    finish_o()
+            do_s[col, h, :, :VAL] = (ot_s[col, h] + stg[part(TWO + h, VAL)]).T.astype(BF)
+
     sum_dq_via(1)
+    start(dq_far(0, 0) + dq_far(0, 1))
     for pr, h in zip((pr0, pr1), HALVES):
         pr[:] = c_in[h].T
-    start(dq_near(5, 0) + dq_near(6, 1))
-    finals = [pltpu.make_async_copy(do_s.at[col, :, :, :VAL], out_o, outs.at[0])]
-    start(finals)
+
+    def finish_dq_pair():
+        copies = local(dq_arrived(1))
+        start(copies)
+        done(copies)
+        for p in HALVES:
+            add_dq(row_slot(RING), p, HALVES)
+
+    finish_dq_pair()
+    start(dq_across(0))
 
     def finish_dkv():
         sums = None
@@ -708,7 +755,7 @@
     finish_dkv()
 
     def w_swap(src, dst, n):
-        return remote([(src, dst)], w_send.at[pl.ds(n, 1)], w_recv.at[pl.ds(n, 1)], mate)
+        return remote([(src, dst)], w_send.at[n], w_recv.at[n], mate, src)
 
     def strip(d):
         return rows_of(d, STRIP)
@@ -721,16 +768,28 @@
         pltpu.make_async_copy(strips, strips, sem.at[n]).wait()
 
     first = w_swap(w_s.at[1 - core], ws_r, 0)
-    start(first + dq_far(0, 0) + dq_far(0, 1))
-
-    def finish_dq_pair():
-        copies = local(dq_arrived(1))
-        start(copies)
-        done(copies)
+    start(first)
+
+    def left_early():
+        left(stats_copies(0, 1))
+        for r in PEERS:
+            left(stats_copies(r, 1))
+            if r != RING:
+                left(o_copies(row_slot(r)))
+            if r % RING in NEIGHBOURS:
+                for p in HALVES:
+                    left(kv_near(r, p))
         for p in HALVES:
-            add_dq(row_slot(RING), p, HALVES)
-
-    finish_dq_pair()
+            left(kv_across(p) + dq_far(1, p))
+            for r in NEIGHBOURS:
+                left(dq_near(RING + r, p))
+            for d in HALVES:
+                left(kv_far(d, p))
+        left(o_pair())
+        for n in range(RING):
+            left(own_copies(*q_kind, n) + own_copies(*k_kind, n))
+        for n in range(FAR):
+            left(pair_copies(*q_kind, n) + pair_copies(*k_kind, n) + pair_copies(*do_kind, n))
 
     def finish_c():
         w_all = jnp.concatenate([wk_in[:], wv_in[:]], axis=1).astype(F32)
@@ -741,8 +800,7 @@
     outputs = [(sc0, out_c.at[0]), (sc1, out_c.at[1]), (rope_s, out_r)]
     more = [pltpu.make_async_copy(src, dst, outs.at[1 + n]) for n, (src, dst) in enumerate(outputs)]
     start(more)
-    finals += more
-
+    finals = more
 
     def w_one():
         landed(first)
@@ -750,10 +808,16 @@
 
     w_one()
     to_all(0, lambda d: wr_s.at[strip(d)], wr_r.at[me])
-    start(dq_across(0) + dq_near(1, 1) + dq_near(2, 0))
+    start(dq_across(1) + dq_near(1, 1) + dq_near(2, 0))
     wr_r[me] = wr_s[strip(me)]
+    finish_o()
+    o_out = [pltpu.make_async_copy(do_s.at[col, :, :, :VAL], out_o, outs.at[0])]
+    start(o_out)
+    finals += o_out
     sum_dq_via(0)
     left(first)
+
+    left_early()
 
     def w_two():
         all_of(strip_recv, 0)
@@ -762,7 +826,7 @@
     w_two()
     mine = w_s.at[core, strip(me)]
     to_all(1, lambda d: mine, mine)
-    start(dq_across(1) + dq_near(1, 0) + dq_near(2, 1))
+    start(dq_near(1, 0) + dq_near(2, 1))
 
     def w_three():
         all_of(strip_recv, 1)
@@ -798,27 +862,21 @@
     q_out = pltpu.make_async_copy(q_out_s, out_q, outs.at[RING + TWO])
     q_out.start()
 
-    left(last)
-    for n in HALVES:
-        all_of(strip_send, n)
-    for r in PEERS:
-        for s in range(GROUP):
-            left(stats_copies(s, r))
-        if r != RING:
-            left(o_copies(row_slot(r)))
-        if r % RING in NEIGHBOURS:
-            for p in HALVES:
-                left(dq_near(r, p) + kv_near(r, p))
-    for p in HALVES:
-        left(dq_across(p) + kv_across(p))
-        for d in HALVES:
-            left(dq_far(d, p) + kv_far(d, p))
-    left(o_pair())
-    for n in range(RING):
-        left(own_copies(*q_kind, n) + own_copies(*k_kind, n))
-    for n in range(FAR):
-        left(pair_copies(*q_kind, n) + pair_copies(*k_kind, n) + pair_copies(*do_kind, n))
-    done(finals + [q_out])
+    def left_late():
+        left(last)
+        for n in HALVES:
+            all_of(strip_send, n)
+        for p in HALVES:
+            left(dq_across(p) + dq_far(0, p))
+            for r in NEIGHBOURS:
+                left(dq_near(r, p))
+
+    left_late()
+
+    def out_done():
+        done(finals + [q_out])
+
+    out_done()
 
 
 def core_call(c, kpe, q, wk, wv, do):
@@ -830,8 +888,8 @@
     f32 = lambda *s: pltpu.VMEM(s, F32)
     packed = pltpu.VMEM((GROUP, HALF, LANES), BF)
 
-    def sum_sems(n):
-        return (dma(GROUP, TWO, n), dma(TWO, TWO, TWO, n), dma(TWO, TWO, n), dma(TWO, TWO, n), dma(TWO, n), dma(TWO, n))
+    def sum_sems():
+        return [dma(*s) for s in ((GROUP, TWO), (TWO, TWO, TWO), (TWO, TWO), (TWO, TWO), (TWO,), (TWO,))]
 
     def sum_bufs(*s):
         return [shape((TWO, TWO, TWO, *s), F32), shape((TWO, TWO, *s), F32), shape((TWO, *s), F32)]
@@ -846,9 +904,8 @@
         f32(TWO, LATENT, NOPE), f32(LATENT, NOPE), f32(LATENT, NOPE), f32(ROPE, TWO * HALF), f32(QK, TWO * HALF),
         f32(LATENT, NOPE), f32(CHIPS, STRIP, NOPE),
         *[f32(*square)] * RING, *[pltpu.VMEM(square, BF)] * RING,
-        dma(len(PEERS), TWO), dma(GROUP, TWO), dma(len(PEERS), 3), dma(GROUP, 3), dma(len(PEERS), 1), dma(GROUP, 1),
-        dma(GROUP, len(PEERS)), dma(GROUP), dma(GROUP, TWO), dma(TWO, RING, TWO), dma(TWO), dma(TWO),
-        sum_sems(3), sum_sems(TWO), dma(GROUP), dma(GROUP), dma(TWO), dma(TWO), dma(TWO), dma(TWO),
+        *[dma(GROUP)] * GROUP, dma(GROUP), dma(TWO, RING), dma(1), dma(1),
+        sum_sems(), sum_sems(), dma(GROUP), dma(GROUP), dma(TWO), dma(TWO), dma(TWO), dma(TWO),
     ]
     results = [
         shape((TWO, HALF, VAL), BF), shape((QK, TWO * HALF), F32), shape((TWO, HALF, LATENT), F32), shape((ROPE, TWO * HALF), F32),

time: 258 us -> 246 us (0.953)
  Pallas kernels: 250 us -> 236 us
    pallas_call x1, Pallas kernels: 250 us -> 236 us  [core_call(): pl.pallas_call(core_kernel, out_shape=results + landing, in_specs=[pl.Blo...]
where the time goes in v4:
time: 246 us; the launch traced here: 244 us
  Pallas kernels  236 us (96%)
  local copies, waits for them, and re-layouts  7.39 us (3%)
    pallas_call x1, Pallas kernels, core_call(): pl.pallas_call(core_kernel, out_shape=results + landing, in_specs=[pl.Blo...  236 us
    unnamed x14, local copies, waits for them, and re-layouts  7.39 us

profile of v4, /device:TPU:1, one launch (start us, length us, event | category | flops | bytes accessed | tf_op | source)
XLA Modules:
  0.0 244.3 jit_solution(12268911344437325500)
XLA Ops:
  0.6 236.3 %core.1 = (bf16[2,512,128]{2,1,0:T(8,128)(2,1)}, f32[192,1024]{1,0:T(8,128)}, f32[2,512,512]{2,1,0:T(8,128)}, f32[64,1024]{1,0:T(8,128)}, f32[512,128]{1,0:T(8,1...) custom-call(bf16[2,512,512]{2,1,0:T(8,128)(2,1)} %bitcast.25, ...), custom_call_target="tpu_custom_call" | custom-call | tf_op jit(solution)/shard_map/core/pallas_call | solution.py:916
  236.9 0.0 copy-start
  236.9 1.8 copy.20
  238.7 0.0 copy-start.3
  238.7 2.1 copy.21
  240.9 0.0 copy-done
  240.9 0.0 copy-start.2
  240.9 0.0 copy-start.1
  240.9 1.3 copy.22
  242.2 0.0 copy-done.3
  242.2 0.7 copy.23
  242.9 0.0 copy-done.2
  242.9 0.7 copy.24
  243.6 0.0 copy-done.1
  243.6 0.7 copy.25
Async XLA Ops:
  236.9 4.0 %copy-start = (f32[2,512,512]{2,1,0:T(8,128)S(1)}, f32[2,512,512]{2,1,0:T(8,128)}, u32[]{:S(2)}) copy-start(f32[2,512,512]{2,1,0:T(8,128)} %get-tuple-element.14) | copy-start | bytes 6291460
  238.7 3.5 %copy-start.3 = (f32[64,1024]{1,0:T(8,128)S(1)}, f32[64,1024]{1,0:T(8,128)}, u32[]{:S(2)}) copy-start(f32[64,1024]{1,0:T(8,128)} %get-tuple-element.15) | copy-start | bytes 786436
  240.9 2.0 copy-start.2
  240.9 2.7 %copy-start.1 = (f32[512,128]{1,0:T(8,128)S(1)}, f32[512,128]{1,0:T(8,128)}, u32[]{:S(2)}) copy-start(f32[512,128]{1,0:T(8,128)} %get-tuple-element.17) | copy-start | bytes 786436

commit v5 on v4

--- a/solution.py
+++ b/solution.py
@@ -33,7 +33,8 @@
 Q_STEPS = (1, 2, 9, 12, 25, 30, 35)
 K_STEPS = (3, 6, 15, 20, 40, 48, 56)
 DO_STEPS, DO_RANKS = (49, 50, 51, 52, 53, 54), (1, 2, 3, 5, 6, 7)
-T_RELAY, T_OWN_DO, T_RELAY_DO = 9, 12, 34
+K_RANKS = (1, 2, 4, 3, 5, 6, 7)
+T_RELAY, T_RELAY_K, T_OWN_DO, T_RELAY_DO = 4, 11, 18, 36
 T_LAST = 56
 T_END = 64
 RECTS = ((1, 0, 1, 1, 2, False), (3, 1, 2, 0, 3, False), (9, 0, 3, 3, 2, True), (15, 3, 2, 0, 5, False), (25, 0, 5, 5, 3, True), (40, 5, 2, 0, 8, False))
@@ -148,9 +149,9 @@
     return near, far, across
 
 
-def core_kernel(c_in, kpe_in, q_in, wk_in, wv_in, do_in,
+def core_kernel(c_arg, kpe_arg, q_arg, wk_arg, wv_arg, do_arg,
                 out_o, out_q, out_c, out_r, out_uk, out_uv, xo, po, xq, xqv, pq, zkv, zkvv, pkv,
-                q_s, qr_s, k_s, kr_s, vt_s, do_s, qt_s, kt_s, dot_s,
+                c_in, kpe_in, q_in, wk_in, wv_in, do_in, q_s, qr_s, k_s, kr_s, vt_s, do_s, qt_s, kt_s, dot_s,
                 ot_s, m_s, l_s, dq_s, dqr_s, dk_s, dv_s, st_s, st_r, stg, w_s, ws_r, wl_r, rope_s, q_out_s, wr_s, wr_r,
                 sc0, sc1, dp0, dp1, pr0, pr1, ds0, ds1,
                 q_send, q_recv, k_send, k_recv, do_send, do_recv, st_send, st_recv, xo_send, xo_recv, po_send, po_recv,
@@ -173,6 +174,8 @@
     def col_dev(rank):
         return {'cp': GROUP * col_slot(rank) + col}
 
+    args = [pltpu.make_async_copy(src, dst, loc.at[n]) for n, (src, dst) in enumerate(((q_arg, q_in), (do_arg, do_in), (kpe_arg, kpe_in), (wv_arg, wv_in), (wk_arg, wk_in), (c_arg, c_in)))]
+    start(args)
     mate = {'data': 1 - core}
     barrier = pltpu.get_barrier_semaphore()
 
@@ -186,6 +189,7 @@
     to_others(lambda d: pl.semaphore_signal(barrier, inc=1, device_id={'cp': d}))
     pl.semaphore_signal(barrier, inc=1, device_id=mate)
 
+    done(args)
     wvt = wv_in[:].T
     for h in HALVES:
         q = q_in[:, part(h, HALF)]
@@ -292,6 +296,7 @@
             pa, pb = (a0 + u % na, b0 + u // na) if inner else (a0 + u // nb, b0 + u % nb)
             a, b = jnp.where(t < end, pa, a), jnp.where(t < end, pb, b)
             end = t0
+        a = jnp.where(a == FAR, RING, jnp.where(a == RING, FAR, a))
         return two_blocks(col_slot(a), jnp.where(t < T_LAST, row_slot(b), t - T_LAST))
 
     def f_scores(sc, blk):
@@ -336,7 +341,7 @@
         st_r[qs, col] = st_s[qs]
 
     def f_arrive(t):
-        @pl.when(among(t, tuple(sorted({*Q_STEPS, *K_STEPS, *DO_STEPS, T_RELAY, T_OWN_DO, T_RELAY_DO}))))
+        @pl.when(among(t, tuple(sorted({*Q_STEPS, *K_STEPS, *DO_STEPS, T_RELAY, T_RELAY_K, T_OWN_DO, T_RELAY_DO}))))
         def _():
             @pl.when(among(t, Q_STEPS))
             def _():
@@ -353,7 +358,7 @@
 
             @pl.when(among(t, K_STEPS))
             def _():
-                rank = at(t, K_STEPS, PEERS)
+                rank = at(t, K_STEPS, K_RANKS)
 
                 @pl.when(rank != RING)
                 def _():
@@ -375,6 +380,9 @@
                 wait_q(RING)
                 for n in range(FAR):
                     start(pair_copies(*q_kind, n))
+
+            @pl.when(t == T_RELAY_K)
+            def _():
                 wait_k(RING)
                 for n in range(FAR):
                     start(pair_copies(*k_kind, n))
@@ -473,7 +481,7 @@
             ot_s[slot, h] = ot_s[slot, h] + sum(stg[HALF * n + h * VAL:HALF * n + (h + 1) * VAL] for n in range(FAR))
 
     def kv_local(d, h):
-        return local([(zkv.at[d, n, h], stg.at[pl.ds(KV * n, KV)]) for n in HALVES])
+        return local([(zkv.at[d, n, h], stg.at[pl.ds(KV * (TWO * h + n), KV)]) for n in HALVES], TWO * h)
 
     def fetch_kv(d, h):
         for r in NEIGHBOURS:
@@ -482,8 +490,10 @@
 
     def add_kv(slot, d, h):
         done(kv_local(d, h))
-        dk_s[slot, h] = dk_s[slot, h] + (stg[:QK] + stg[KV:KV + QK])
-        dv_s[slot, h] = dv_s[slot, h] + (stg[QK:KV] + stg[KV + QK:KV + KV])
+        u = KV * TWO * h
+        v = u + KV
+        dk_s[slot, h] = dk_s[slot, h] + (stg[u:u + QK] + stg[v:v + QK])
+        dv_s[slot, h] = dv_s[slot, h] + (stg[u + QK:v] + stg[v + QK:v + KV])
 
     def kv_via_local(d):
         return local([(zkvv.at[d, h], stg.at[pl.ds(KV * h, KV)]) for h in HALVES])
@@ -537,8 +547,13 @@
     def wait_stats(qs):
         landed(stats_copies(qs, 1))
 
+    def prepare_two(qs):
+        for n in HALVES:
+            wait_stats(qs + n)
+        for n in HALVES:
+            prepare(qs + n)
+
     def prepare(qs):
-        wait_stats(qs)
         m, l, d = (st_r[qs, :, part(i, GROUP)] for i in range(3))
         m_all = jnp.max(m, axis=0)
         w = jnp.exp2((m - m_all[None]) * EXP2_SCALE)
@@ -602,8 +617,7 @@
         def _():
             @pl.when((t < GROUP - 1) & (t % TWO == 1))
             def _():
-                for n in NEIGHBOURS:
-                    prepare(t + n)
+                prepare_two(t + 1)
 
             @pl.when((t <= GROUP) & ((t - 1) % RING != x))
             def _():
@@ -691,8 +705,7 @@
 
     for ref in (pr1, ds1):
         ref[:] = jnp.zeros(ref.shape, BF)
-    for s in HALVES:
-        prepare(s)
+    prepare_two(0)
     blocks = b_blocks(jnp.int32(0))
     b_scores(sc0, dp0, blocks[0])
     before, _ = lax.fori_loop(0, T_END - 1, b_step, (blocks[1], blocks))
@@ -719,7 +732,7 @@
             do_s[col, h, :, :VAL] = (ot_s[col, h] + stg[part(TWO + h, VAL)]).T.astype(BF)
 
     sum_dq_via(1)
-    start(dq_far(0, 0) + dq_far(0, 1))
+    start(dq_far(0, 0) + dq_far(0, 1) + dq_near(1, 1) + dq_near(2, 0))
     for pr, h in zip((pr0, pr1), HALVES):
         pr[:] = c_in[h].T
 
@@ -735,15 +748,17 @@
 
     def finish_dkv():
         sums = None
+        pair = local([(pkv.at[h], sc.at[pl.ds(0, KV)]) for h, sc in enumerate((sc0, sc1))], RING)
+        for h in HALVES:
+            landed(kv_across(h))
+        start(pair)
         for h in HALVES:
             fetch_kv(0, h)
-            landed(kv_across(h))
-            pair = local([(pkv.at[h], sc0.at[pl.ds(0, KV)])], TWO)
-            start(pair)
+        done(pair)
+        for h, sc in enumerate((sc0, sc1)):
             add_kv(row, 0, h)
-            done(pair)
-            dk = (dk_s[row, h] + sc0[:QK]) * SCALE
-            dv = dv_s[row, h] + sc0[QK:KV]
+            dk = (dk_s[row, h] + sc[:QK]) * SCALE
+            dv = dv_s[row, h] + sc[QK:KV]
             rope_s[:, part(h, HALF)] = dk[NOPE:]
             kv = jnp.concatenate([dk[:NOPE].T, dv.T], axis=1)
             (dp0, dp1)[h][:, :NOPE + VAL] = kv
@@ -808,13 +823,14 @@
 
     w_one()
     to_all(0, lambda d: wr_s.at[strip(d)], wr_r.at[me])
-    start(dq_across(1) + dq_near(1, 1) + dq_near(2, 0))
+    start(dq_across(1))
     wr_r[me] = wr_s[strip(me)]
+    sum_dq_via(0)
+    start(dq_near(1, 0) + dq_near(2, 1))
     finish_o()
     o_out = [pltpu.make_async_copy(do_s.at[col, :, :, :VAL], out_o, outs.at[0])]
     start(o_out)
     finals += o_out
-    sum_dq_via(0)
     left(first)
 
     left_early()
@@ -826,7 +842,6 @@
     w_two()
     mine = w_s.at[core, strip(me)]
     to_all(1, lambda d: mine, mine)
-    start(dq_near(1, 0) + dq_near(2, 1))
 
     def w_three():
         all_of(strip_recv, 1)
@@ -895,7 +910,7 @@
         return [shape((TWO, TWO, TWO, *s), F32), shape((TWO, TWO, *s), F32), shape((TWO, *s), F32)]
 
     square = (HALF, HALF)
-    scratch = [
+    scratch = [pltpu.VMEM(a.shape, a.dtype) for a in (c, kpe, q, wk, wv, do)] + [
         wide(HALF, QK + AUG), packed, wide(HALF, QK + ROPE), packed, wide(VAL + AUG, HALF), wide(HALF, VAL + AUG),
         wide(QK, HALF), wide(QK + AUG, HALF), wide(VAL, HALF),
         sums(VAL, HALF), sums(1, HALF), sums(1, HALF),
@@ -916,7 +931,7 @@
     return pl.pallas_call(
         core_kernel,
         out_shape=results + landing,
-        in_specs=[pl.BlockSpec(memory_space=pltpu.VMEM)] * 6,
+        in_specs=[anywhere] * 6,
         out_specs=[anywhere] * len(results + landing),
         scratch_shapes=scratch,
         compiler_params=pltpu.CompilerParams(collective_id=0, has_side_effects=True, vmem_limit_bytes=67043328),

time: 246 us -> 241 us (0.980)
  Pallas kernels: 236 us -> 233 us
    pallas_call x1, Pallas kernels: 236 us -> 233 us  [core_call(): pl.pallas_call(core_kernel, out_shape=results + landing, in_specs=[anywhe...]
where the time goes in v5:
time: 241 us
  Pallas kernels  233 us (97%)
  local copies, waits for them, and re-layouts  7.39 us (3%)
    pallas_call x1, Pallas kernels, core_call(): pl.pallas_call(core_kernel, out_shape=results + landing, in_specs=[anywhe...  233 us
    unnamed x14, local copies, waits for them, and re-layouts  7.39 us

profile of v5, /device:TPU:1, one launch (start us, length us, event | category | flops | bytes accessed | tf_op | source)
XLA Modules:
  0.0 241.0 jit_solution(16922570123575173595)
XLA Ops:
  0.6 232.9 %core.1 = (bf16[2,512,128]{2,1,0:T(8,128)(2,1)}, f32[192,1024]{1,0:T(8,128)}, f32[2,512,512]{2,1,0:T(8,128)}, f32[64,1024]{1,0:T(8,128)}, f32[512,128]{1,0:T(8,1...) custom-call(bf16[2,512,512]{2,1,0:T(8,128)(2,1)} %bitcast.25, ...), custom_call_target="tpu_custom_call" | custom-call | tf_op jit(solution)/shard_map/core/pallas_call | solution.py:931
  233.6 0.0 copy-start
  233.6 1.8 copy.20
  235.4 0.0 copy-start.3
  235.4 2.1 copy.21
  237.5 0.0 copy-done
  237.5 0.0 copy-start.2
  237.5 0.0 copy-start.1
  237.5 1.3 copy.22
  238.8 0.0 copy-done.3
  238.8 0.7 copy.23
  239.6 0.0 copy-done.2
  239.6 0.7 copy.24
  240.3 0.0 copy-done.1
  240.3 0.7 copy.25
Async XLA Ops:
  233.6 4.0 %copy-start = (f32[2,512,512]{2,1,0:T(8,128)S(1)}, f32[2,512,512]{2,1,0:T(8,128)}, u32[]{:S(2)}) copy-start(f32[2,512,512]{2,1,0:T(8,128)} %get-tuple-element.14) | copy-start | bytes 6291460
  235.4 3.5 %copy-start.3 = (f32[64,1024]{1,0:T(8,128)S(1)}, f32[64,1024]{1,0:T(8,128)}, u32[]{:S(2)}) copy-start(f32[64,1024]{1,0:T(8,128)} %get-tuple-element.15) | copy-start | bytes 786436
  237.5 2.0 copy-start.2
  237.5 2.7 %copy-start.1 = (f32[512,128]{1,0:T(8,128)S(1)}, f32[512,128]{1,0:T(8,128)}, u32[]{:S(2)}) copy-start(f32[512,128]{1,0:T(8,128)} %get-tuple-element.17) | copy-start | bytes 786436

commit v6 on v5

--- a/solution.py
+++ b/solution.py
@@ -40,16 +40,16 @@
 RECTS = ((1, 0, 1, 1, 2, False), (3, 1, 2, 0, 3, False), (9, 0, 3, 3, 2, True), (15, 3, 2, 0, 5, False), (25, 0, 5, 5, 3, True), (40, 5, 2, 0, 8, False))
 K_ORDER = (7, 5, 6, 4, 3, 1, 2)
 Q_FIRST, Q_REST = (7, 5, 6), (3, 1, 2, 4, 0)
-T_SPLIT, T_MIX = 48, 52
-M_REST, M_OWN = 9, 14
+T_MIX = 48
+M_NEAR, M_FAR, M_OWN = 12, 17, 22
 T_VIA = (9, 41)
 T_FETCH, T_ADD = (21, 53), (22, 54)
 T_NEAR, NEAR = (23, 25), (5, 6)
 T_ONE = (49, 55)
-T_NEAR_MID, T_NEAR_LAST = 55, 60
+T_NEAR_MID, T_NEAR_LAST = 57, 60
 T_PAIR_O = 56
 T_PAIR_KV = (36, 45)
-T_VIA_Q, T_Q_FIVE, T_Q_SIX = 54, 56, 57
+T_VIA_Q, T_Q_FIVE, T_Q_SIX = 51, 53, 55
 
 
 def mm(a, b):
@@ -150,7 +150,7 @@
 
 
 def core_kernel(c_arg, kpe_arg, q_arg, wk_arg, wv_arg, do_arg,
-                out_o, out_q, out_c, out_r, out_uk, out_uv, xo, po, xq, xqv, pq, zkv, zkvv, pkv,
+                out_o, out_q, out_c, out_r, out_w, xo, po, xq, xqv, pq, zkv, zkvv, pkv,
                 c_in, kpe_in, q_in, wk_in, wv_in, do_in, q_s, qr_s, k_s, kr_s, vt_s, do_s, qt_s, kt_s, dot_s,
                 ot_s, m_s, l_s, dq_s, dqr_s, dk_s, dv_s, st_s, st_r, stg, w_s, ws_r, wl_r, rope_s, q_out_s, wr_s, wr_r,
                 sc0, sc1, dp0, dp1, pr0, pr1, ds0, ds1,
@@ -570,21 +570,19 @@
                 ot_s[qs, h, :, c] = ot_s[qs, h, :, c] * mine[part(BLOCKS * h + j, 1)]
 
     def b_mixed(m):
-        first, rest = m < M_REST, m < M_OWN
-        rank = jnp.where(first, order(m // 3, Q_FIRST), order(jnp.where(rest, m - M_REST, (m - M_OWN) // TWO), Q_REST))
-        ring = jnp.where(first, m % 3, jnp.where(rest, 0, 1)) == 0
-        same = ring | (jnp.where(first, m % 3, 1 + m % TWO) == TWO)
-        ks, qs = jnp.where(ring, col_slot(K_ORDER[-1]), row), row_slot(rank)
+        first, near, far = m < M_NEAR, m < M_FAR, m < M_OWN
+        rest = jnp.where(near, m - M_NEAR, jnp.where(far, m - M_FAR, (m - M_OWN) // TWO))
+        qs = row_slot(jnp.where(first, order(m // RING, Q_FIRST), order(rest, Q_REST)))
+        kind = jnp.where(first, m % RING, jnp.where(near, 0, jnp.where(far, 1, TWO + m % TWO)))
+        ks = jnp.where(kind < TWO, col_slot(K_ORDER[-1]), row)
+        same = kind % TWO == 1
         h = diagonal_half(ks, qs)
         return ks, qs, jnp.where(same, h, 0), jnp.where(same, h, 1)
 
     def b_blocks(t):
-        b1, b2 = two_blocks(col_slot(order(t // GROUP, K_ORDER)), t % GROUP)
-        pick = lambda c, a, b: tuple(jnp.where(c, i, j) for i, j in zip(a, b))
-        last = col_slot(K_ORDER[-1])
-        u = TWO * (t - T_SPLIT)
-        m = TWO * (t - T_MIX)
-        return tuple(pick(t < T_SPLIT, b, pick(t < T_MIX, (last, u + n, 0, 1), b_mixed(m + n))) for n, b in enumerate((b1, b2)))
+        pick = lambda a, b: tuple(jnp.where(t < T_MIX, i, j) for i, j in zip(a, b))
+        plain = two_blocks(col_slot(order(t // GROUP, K_ORDER)), t % GROUP)
+        return tuple(pick(b, b_mixed(TWO * (t - T_MIX) + n)) for n, b in enumerate(plain))
 
     def b_scores(sc, dp, blk):
         ks, qs, kh, qh = blk
@@ -709,6 +707,7 @@
     blocks = b_blocks(jnp.int32(0))
     b_scores(sc0, dp0, blocks[0])
     before, _ = lax.fori_loop(0, T_END - 1, b_step, (blocks[1], blocks))
+    start(dq_near(1, 1) + dq_near(2, 0))
     b_grads(pr1, ds1, before)
 
     def own_b():
@@ -732,7 +731,7 @@
             do_s[col, h, :, :VAL] = (ot_s[col, h] + stg[part(TWO + h, VAL)]).T.astype(BF)
 
     sum_dq_via(1)
-    start(dq_far(0, 0) + dq_far(0, 1) + dq_near(1, 1) + dq_near(2, 0))
+    start(dq_far(0, 0) + dq_far(0, 1))
     for pr, h in zip((pr0, pr1), HALVES):
         pr[:] = c_in[h].T
 
@@ -811,12 +810,6 @@
         for kv, out in ((dp0, sc0), (dp1, sc1)):
             out[:] = mm_t(kv[:, :NOPE + VAL], w_all)
 
-    finish_c()
-    outputs = [(sc0, out_c.at[0]), (sc1, out_c.at[1]), (rope_s, out_r)]
-    more = [pltpu.make_async_copy(src, dst, outs.at[1 + n]) for n, (src, dst) in enumerate(outputs)]
-    start(more)
-    finals = more
-
     def w_one():
         landed(first)
         wr_s[:] = w_s[core] + ws_r[:]
@@ -828,9 +821,10 @@
     sum_dq_via(0)
     start(dq_near(1, 0) + dq_near(2, 1))
     finish_o()
-    o_out = [pltpu.make_async_copy(do_s.at[col, :, :, :VAL], out_o, outs.at[0])]
-    start(o_out)
-    finals += o_out
+    finish_c()
+    outputs = [(do_s.at[col, :, :, :VAL], out_o), (sc0, out_c.at[0]), (sc1, out_c.at[1]), (rope_s, out_r)]
+    finals = [pltpu.make_async_copy(src, dst, outs.at[n]) for n, (src, dst) in enumerate(outputs)]
+    start(finals)
     left(first)
 
     left_early()
@@ -842,13 +836,6 @@
     w_two()
     mine = w_s.at[core, strip(me)]
     to_all(1, lambda d: mine, mine)
-
-    def w_three():
-        all_of(strip_recv, 1)
-
-    w_three()
-    last = w_swap(w_s.at[core], wl_r, 1)
-    start(last)
 
     def finish_dq():
         pairs = dq_arrived(0)
@@ -865,20 +852,19 @@
         for h in HALVES:
             q_out_s[NOPE:, part(h, HALF)] = rope[part(h, ROPE)]
 
-    def w_five():
-        landed(last)
-        w_s[1 - core] = wl_r[:]
-
-    w_five()
-    more = [pltpu.make_async_copy(src, dst, outs.at[RING + n]) for n, (src, dst) in enumerate([(w_s.at[0], out_uk), (w_s.at[1], out_uv)])]
-    start(more)
-    finals += more
     finish_dq()
-    q_out = pltpu.make_async_copy(q_out_s, out_q, outs.at[RING + TWO])
-    q_out.start()
+    q_out = [pltpu.make_async_copy(q_out_s, out_q, outs.at[RING])]
+    start(q_out)
+
+    def w_three():
+        all_of(strip_recv, 1)
+
+    w_three()
+    last = w_swap(w_s.at[core], wl_r, 1)
+    own_w = [pltpu.make_async_copy(w_s.at[core], out_w.at[core], outs.at[RING + 1])]
+    start(last + own_w)
 
     def left_late():
-        left(last)
         for n in HALVES:
             all_of(strip_send, n)
         for p in HALVES:
@@ -889,7 +875,11 @@
     left_late()
 
     def out_done():
-        done(finals + [q_out])
+        landed(last)
+        mate_w = [pltpu.make_async_copy(wl_r, out_w.at[1 - core], outs.at[RING + TWO])]
+        start(mate_w)
+        left(last)
+        done(finals + q_out + own_w + mate_w)
 
     out_done()
 
@@ -924,7 +914,7 @@
     ]
     results = [
         shape((TWO, HALF, VAL), BF), shape((QK, TWO * HALF), F32), shape((TWO, HALF, LATENT), F32), shape((ROPE, TWO * HALF), F32),
-        shape((LATENT, NOPE), F32), shape((LATENT, VAL), F32),
+        shape((TWO, LATENT, NOPE), F32),
     ]
     landing = [shape((TWO, RING, TWO * VAL, HALF), F32), shape((TWO * VAL, HALF), F32), *sum_bufs(ROWS, 3 * LANES), *sum_bufs(KV, HALF)]
     anywhere = pl.BlockSpec(memory_space=pl.ANY)
@@ -946,7 +936,7 @@
 
     def per_device(c_latent, k_rope, queries, w_uk, w_uv, d_out):
         halves = lambda a: a.reshape(TWO, HALF, a.shape[-1])
-        o, gq, gc, gr, guk, guv = core_call(halves(c_latent), k_rope[0].T, queries[0, :, 0].T, w_uk[:, 0], w_uv[:, 0], halves(d_out))
-        return o.reshape(d_out.shape), gq.T.reshape(queries.shape), gc.reshape(c_latent.shape), gr.T.reshape(k_rope.shape), guk[:, None], guv[:, None]
+        o, gq, gc, gr, gw = core_call(halves(c_latent), k_rope[0].T, queries[0, :, 0].T, w_uk[:, 0], w_uv[:, 0], halves(d_out))
+        return o.reshape(d_out.shape), gq.T.reshape(queries.shape), gc.reshape(c_latent.shape), gr.T.reshape(k_rope.shape), gw[0, :, None], gw[1, :, None]
 
     return jax.shard_map(per_device, mesh=mesh, in_specs=(token_spec, token_spec, token_spec, P(), P(), token_spec), out_specs=(token_spec, token_spec, token_spec, token_spec, sum_spec, sum_spec), check_vma=False)

time: 241 us -> 239 us (level)
  Pallas kernels: 233 us -> 230 us
    pallas_call x1, Pallas kernels: 233 us -> 230 us  [core_call(): pl.pallas_call(core_kernel, out_shape=results + landing, in_specs=[anywhe...]
    unnamed x14 -> x8, local copies, waits for them, and re-layouts: 7.39 us -> 5.83 us
where the time goes in v6:
time: 239 us; the launch traced here: 238 us
  Pallas kernels  230 us (96%)
  local copies, waits for them, and re-layouts  7.83 us (3%)
    pallas_call x1, Pallas kernels, core_call(): pl.pallas_call(core_kernel, out_shape=results + landing, in_specs=[anywhe...  230 us
    unnamed x8, local copies, waits for them, and re-layouts  5.83 us

profile of v6, /device:TPU:1, one launch (start us, length us, event | category | flops | bytes accessed | tf_op | source)
XLA Modules:
  0.0 238.3 jit_solution(14565824118804424764)
XLA Ops:
  0.6 229.8 %core.1 = (bf16[2,512,128]{2,1,0:T(8,128)(2,1)}, f32[192,1024]{1,0:T(8,128)}, f32[2,512,512]{2,1,0:T(8,128)}, f32[64,1024]{1,0:T(8,128)}, f32[2,512,128]{2,1,0:T...) custom-call(bf16[2,512,512]{2,1,0:T(8,128)(2,1)} %bitcast.25, ...), custom_call_target="tpu_custom_call" | custom-call | tf_op jit(solution)/shard_map/core/pallas_call | solution.py:921
  230.4 0.0 copy-start
  230.4 2.0 fusion
  232.4 1.7 copy.18
  234.1 0.0 copy-start.1
  234.1 2.1 copy.19
  236.2 0.0 copy-done
  236.2 1.3 copy.20
  237.6 0.0 copy-done.1
  237.6 0.7 copy.21
Async XLA Ops:
  230.4 5.8 %copy-start = (f32[2,512,512]{2,1,0:T(8,128)S(1)}, f32[2,512,512]{2,1,0:T(8,128)}, u32[]{:S(2)}) copy-start(f32[2,512,512]{2,1,0:T(8,128)} %get-tuple-element.13) | copy-start | bytes 6291460
  234.1 3.5 %copy-start.1 = (f32[64,1024]{1,0:T(8,128)S(1)}, f32[64,1024]{1,0:T(8,128)}, u32[]{:S(2)}) copy-start(f32[64,1024]{1,0:T(8,128)} %get-tuple-element.14) | copy-start | bytes 786436

commit v7 on v6

--- a/solution.py
+++ b/solution.py
@@ -196,7 +196,6 @@
         qt_s[col, h] = q
         q_s[col, h, :, :QK] = q.T
         qr_s[col, :, part(h, ROPE)] = q[NOPE:].T
-        do_s[col, h, :, :VAL] = do_in[h]
     for h in HALVES:
         k_s[row, h, :, :NOPE] = mm(c_in[h], wk_in[:]).astype(BF)
         rope = kpe_in[:, part(h, HALF)].T
@@ -276,6 +275,8 @@
 
     for h in HALVES:
         kt_s[row, h, :QK] = k_s[row, h, :, :QK].T
+    for h in HALVES:
+        do_s[col, h, :, :VAL] = do_in[h]
     place_do(col)
     lax.fori_loop(0, GROUP, clear, 0)
 
@@ -340,8 +341,11 @@
             start(stats_copies(qs, n))
         st_r[qs, col] = st_s[qs]
 
+    def f_event(t):
+        return among(t, tuple(sorted({*Q_STEPS, *K_STEPS, *DO_STEPS, T_RELAY, T_RELAY_K, T_OWN_DO, T_RELAY_DO})))
+
     def f_arrive(t):
-        @pl.when(among(t, tuple(sorted({*Q_STEPS, *K_STEPS, *DO_STEPS, T_RELAY, T_RELAY_K, T_OWN_DO, T_RELAY_DO}))))
+        @pl.when(f_event(t))
         def _():
             @pl.when(among(t, Q_STEPS))
             def _():
@@ -407,20 +411,23 @@
 
     def f_half(t, used, made, b1, b2):
         n1, n2 = after = f_blocks(jnp.minimum(t + 1, T_END - 1))
+        eventful = f_event(t + TWO) | (t >= T_LAST)
         f_scores(made[0], n1)
         f_use(used[0], b1)
         f_scores(made[1], n2)
         f_use(used[1], b2)
 
-        @pl.when(t >= T_LAST)
+        @pl.when(eventful)
         def _():
-            @pl.when(t > T_LAST)
-            def _():
-                start_stats(t - T_LAST - 1)
-
-            make_stats(t - T_LAST)
-
-        f_arrive(t + TWO)
+            @pl.when(t >= T_LAST)
+            def _():
+                @pl.when(t > T_LAST)
+                def _():
+                    start_stats(t - T_LAST - 1)
+
+                make_stats(t - T_LAST)
+
+            f_arrive(t + TWO)
         return after
 
     def f_step(u, carry):

time: 239 us -> 238 us (level)
  no operation moved by 1% of the time
where the time goes in v7:
time: 238 us
  Pallas kernels  229 us (96%)
  local copies, waits for them, and re-layouts  7.83 us (3%)
    pallas_call x1, Pallas kernels, core_call(): pl.pallas_call(core_kernel, out_shape=results + landing, in_specs=[anywhe...  229 us
    unnamed x8, local copies, waits for them, and re-layouts  5.83 us

profile of v7, /device:TPU:1, one launch (start us, length us, event | category | flops | bytes accessed | tf_op | source)
XLA Modules:
  0.0 237.8 jit_solution(10830404256519087841)
XLA Ops:
  0.6 229.3 %core.1 = (bf16[2,512,128]{2,1,0:T(8,128)(2,1)}, f32[192,1024]{1,0:T(8,128)}, f32[2,512,512]{2,1,0:T(8,128)}, f32[64,1024]{1,0:T(8,128)}, f32[2,512,128]{2,1,0:T...) custom-call(bf16[2,512,512]{2,1,0:T(8,128)(2,1)} %bitcast.25, ...), custom_call_target="tpu_custom_call" | custom-call | tf_op jit(solution)/shard_map/core/pallas_call | solution.py:928
  230.0 0.0 copy-start
  230.0 2.0 fusion
  232.0 1.7 copy.18
  233.7 0.0 copy-start.1
  233.7 2.1 copy.19
  235.8 0.0 copy-done
  235.8 1.3 copy.20
  237.1 0.0 copy-done.1
  237.1 0.7 copy.21
Async XLA Ops:
  230.0 5.8 %copy-start = (f32[2,512,512]{2,1,0:T(8,128)S(1)}, f32[2,512,512]{2,1,0:T(8,128)}, u32[]{:S(2)}) copy-start(f32[2,512,512]{2,1,0:T(8,128)} %get-tuple-element.13) | copy-start | bytes 6291460
  233.7 3.5 %copy-start.1 = (f32[64,1024]{1,0:T(8,128)S(1)}, f32[64,1024]{1,0:T(8,128)}, u32[]{:S(2)}) copy-start(f32[64,1024]{1,0:T(8,128)} %get-tuple-element.14) | copy-start | bytes 786436
